TPU v7x, 32 devices: a whole 2x2x4 slice. The times are simulated.
32 devices in a mesh: dp: 4 (over y, x), bins: 8 (over z, core).
Axes of the slice: x: 2, y: 2, z: 4, core: 2. Of those that a mesh axis runs over, the one named last changes fastest.
Arguments:
- activations: bfloat16 [64, 1024, 768], P('dp', 'bins'), may hold values from -16 to 16
- shift_bins: int32 [64], P('dp'), may hold values from -3 to 3, as said below
- reverse_flags: int32 [64], P('dp'), may hold values from 0 to 1
- gain_one: bfloat16 [768], P('bins'), may hold values from 0.5 to 1.5
- bias_one: bfloat16 [768], P('bins'), may hold values from -3 to 3
- conv_weight: bfloat16 [3, 768, 384], P(None, 'bins'), may hold values from -0.125 to 0.125
- gain_two: bfloat16 [384], P('bins'), may hold values from 0.5 to 1.5
- bias_two: bfloat16 [384], P('bins'), may hold values from -3 to 3
- proj_weight: bfloat16 [384, 768], P(None, 'bins'), may hold values from -0.3125 to 0.3125
- proj_bias: bfloat16 [768], P('bins'), may hold values from -2 to 2
- cotangent: bfloat16 [64, 1024, 768], P('dp', 'bins'), may hold values from -6 to 6
Outputs:
- output: bfloat16 [64, 1024, 768], P('dp', 'bins')
- grad_activations: bfloat16 [64, 1024, 768], P('dp', 'bins')
- grad_gain_one: float32 [768], P(('dp', 'bins'))
- grad_bias_one: float32 [768], P(('dp', 'bins'))
- grad_conv_weight: float32 [3, 768, 384], P(None, ('dp', 'bins'))
- grad_gain_two: float32 [384], P('bins')
- grad_bias_two: float32 [384], P('bins')
- grad_proj_weight: float32 [384, 768], P(None, ('dp', 'bins'))
- grad_proj_bias: float32 [768], P(('dp', 'bins'))
Inputs may be any that keep to these rules, and one draw needn't show every extreme that they name: `shift_bins`: both 3 and -3 occur in every draw.
All inputs are finite; a program needn't handle non-finite values.
Results may differ from a plain program's by a relative error of at most 0.0067.
Values may be sent and summed in bfloat16 or wider, within the bound.
A program may use at most 128 MiB of HBM per device.

v0:
```python
import jax
import jax.numpy as jnp
from jax import lax
from jax.sharding import PartitionSpec as P

KERNEL_TAPS = 3
DILATION_BINS = 8
SHIFT = 3
MICRO = 4


EPSILON = 1e-05


def partner(value, axis, apart):
    mask = 2**apart
    pairs = [(source, source ^ mask) for source in range(lax.axis_size(axis))]
    return lax.ppermute(value, axis, pairs)


def with_halo(block, sides, width):
    for axis, dim in sides:
        count = lax.axis_size(axis)
        forward = [(i, i + 1) for i in range(count - 1)]
        backward = [(target, source) for source, target in forward]
        low = lax.ppermute(
            lax.slice_in_dim(block, block.shape[dim] - width, None, axis=dim), axis, forward
        )
        high = lax.ppermute(lax.slice_in_dim(block, 0, width, axis=dim), axis, backward)
        block = jnp.concatenate([low, block, high], axis=dim)
    return block


def gelu_plain(values):
    return jax.nn.gelu(values, approximate=True)


def gelu_back(values, upstream):
    return jax.vjp(gelu_plain, values)[1](upstream)[0]


def shift_sequences(padded_rows, starts, count_of_rows):
    return jax.vmap(
        lambda sequence, starting_row: lax.dynamic_slice_in_dim(
            sequence, starting_row, count_of_rows, 0
        )
    )(padded_rows, starts)


def move_forward(values, offsets, reverse_mask):
    count_of_rows = values.shape[1]
    flipped = values
    for bit_index in range(lax.axis_size("bins").bit_length() - 1):
        flipped = partner(flipped, "bins", bit_index)
    flipped = jnp.flip(flipped, axis=1)
    chosen = jnp.where(reverse_mask[:, None, None], flipped, values)
    padded_rows = with_halo(chosen, (("bins", 1),), SHIFT)
    return shift_sequences(padded_rows, SHIFT - offsets, count_of_rows)


def move_backward(values, offsets, reverse_mask):
    count_of_rows = values.shape[1]
    flipped = values
    for bit_index in range(lax.axis_size("bins").bit_length() - 1):
        flipped = partner(flipped, "bins", bit_index)
    flipped = jnp.flip(flipped, axis=1)
    chosen = jnp.where(reverse_mask[:, None, None], flipped, values)
    padded_rows = with_halo(chosen, (("bins", 1),), SHIFT)
    return shift_sequences(padded_rows, SHIFT - offsets, count_of_rows)


def gather_weights(gain_one, bias_one, conv_weight, gain_two, bias_two, proj_weight, proj_bias):
    return (
        lax.all_gather(gain_one, "bins", axis=0, tiled=True),
        lax.all_gather(bias_one, "bins", axis=0, tiled=True),
        lax.all_gather(conv_weight, "bins", axis=1, tiled=True),
        lax.all_gather(gain_two, "bins", axis=0, tiled=True),
        lax.all_gather(bias_two, "bins", axis=0, tiled=True),
        lax.all_gather(proj_weight, "bins", axis=1, tiled=True),
        lax.all_gather(proj_bias, "bins", axis=0, tiled=True),
    )


def spread(stat):
    return stat[:, None, None, :]


def run_block(moved_block, cot_block, weights):
    gain_one, bias_one, conv_weight, gain_two, bias_two, proj_weight, proj_bias = weights
    scale_one = gain_one.astype(jnp.float32)
    offset_one = bias_one.astype(jnp.float32)
    scale_two = gain_two.astype(jnp.float32)
    offset_two = bias_two.astype(jnp.float32)
    bias_out = proj_bias.astype(jnp.float32)
    count_of_rows = moved_block.shape[2]
    total_rows = moved_block.shape[1] * count_of_rows * lax.axis_size("dp") * lax.axis_size("bins")
    inputs = moved_block.astype(jnp.float32)
    sums_one = lax.psum(
        (jnp.sum(inputs, axis=(1, 2)), jnp.sum(inputs * inputs, axis=(1, 2))), ("dp", "bins")
    )
    mean_one = sums_one[0] / total_rows
    inverse_one = lax.rsqrt(sums_one[1] / total_rows - mean_one * mean_one + EPSILON)
    centred_one = (inputs - spread(mean_one)) * spread(inverse_one)
    normed_one = centred_one * scale_one + offset_one
    first_hidden = gelu_plain(normed_one).astype(jnp.bfloat16)
    first_padded = with_halo(first_hidden, (("bins", 2),), DILATION_BINS)
    conv_out = jnp.zeros(first_hidden.shape[:3] + (conv_weight.shape[2],), jnp.float32)
    for kernel_tap_index in range(KERNEL_TAPS):
        sliding_window = first_padded[
            :,
            :,
            kernel_tap_index * DILATION_BINS : kernel_tap_index * DILATION_BINS + count_of_rows,
        ]
        conv_out = conv_out + jnp.einsum(
            "mblc,cf->mblf",
            sliding_window,
            conv_weight[kernel_tap_index],
            preferred_element_type=jnp.float32,
        )
    sums_two = lax.psum(
        (jnp.sum(conv_out, axis=(1, 2)), jnp.sum(conv_out * conv_out, axis=(1, 2))), ("dp", "bins")
    )
    mean_two = sums_two[0] / total_rows
    inverse_two = lax.rsqrt(sums_two[1] / total_rows - mean_two * mean_two + EPSILON)
    centred_two = (conv_out - spread(mean_two)) * spread(inverse_two)
    normed_two = centred_two * scale_two + offset_two
    hidden_two = gelu_plain(normed_two).astype(jnp.bfloat16)
    branch = (
        jnp.einsum("mblf,fc->mblc", hidden_two, proj_weight, preferred_element_type=jnp.float32)
        + bias_out
    )
    output_block = (inputs + branch).astype(jnp.bfloat16)
    upstream = cot_block.astype(jnp.float32)
    grad_bias = jnp.sum(upstream, axis=(0, 1, 2))
    grad_proj = jnp.einsum(
        "mblf,mblc->fc", hidden_two, cot_block, preferred_element_type=jnp.float32
    )
    grad_hidden_two = jnp.einsum(
        "mblc,fc->mblf", cot_block, proj_weight, preferred_element_type=jnp.float32
    )
    grad_normed_two = gelu_back(normed_two, grad_hidden_two)
    back_two = lax.psum(
        (
            jnp.sum(grad_normed_two, axis=(1, 2)),
            jnp.sum(grad_normed_two * centred_two, axis=(1, 2)),
        ),
        ("dp", "bins"),
    )
    grad_conv = spread(inverse_two * scale_two) * (
        grad_normed_two
        - spread(back_two[0] / total_rows)
        - centred_two * spread(back_two[1] / total_rows)
    )
    gradient_conv_reduced = grad_conv.astype(jnp.bfloat16)
    conv_grads = []
    for kernel_tap_index in range(KERNEL_TAPS):
        sliding_window = first_padded[
            :,
            :,
            kernel_tap_index * DILATION_BINS : kernel_tap_index * DILATION_BINS + count_of_rows,
        ]
        conv_grads.append(
            jnp.einsum(
                "mblc,mblf->cf",
                sliding_window,
                gradient_conv_reduced,
                preferred_element_type=jnp.float32,
            )
        )
    grad_conv_weight = jnp.stack(conv_grads)
    padded_cotangent = with_halo(gradient_conv_reduced, (("bins", 2),), DILATION_BINS)
    grad_hidden_one = jnp.zeros(first_hidden.shape, jnp.float32)
    for kernel_tap_index in range(KERNEL_TAPS):
        starting_row = (KERNEL_TAPS - 1 - kernel_tap_index) * DILATION_BINS
        sliding_window = padded_cotangent[:, :, starting_row : starting_row + count_of_rows]
        grad_hidden_one = grad_hidden_one + jnp.einsum(
            "mblf,cf->mblc",
            sliding_window,
            conv_weight[kernel_tap_index],
            preferred_element_type=jnp.float32,
        )
    grad_normed_one = gelu_back(normed_one, grad_hidden_one)
    back_one = lax.psum(
        (
            jnp.sum(grad_normed_one, axis=(1, 2)),
            jnp.sum(grad_normed_one * centred_one, axis=(1, 2)),
        ),
        ("dp", "bins"),
    )
    grad_inputs = upstream + spread(inverse_one * scale_one) * (
        grad_normed_one
        - spread(back_one[0] / total_rows)
        - centred_one * spread(back_one[1] / total_rows)
    )
    partials = (
        jnp.sum(back_one[1], axis=0),
        jnp.sum(back_one[0], axis=0),
        grad_conv_weight,
        jnp.sum(back_two[1], axis=0),
        jnp.sum(back_two[0], axis=0),
        grad_proj,
        grad_bias,
    )
    return (output_block, grad_inputs.astype(jnp.bfloat16), partials)


def local(
    activations,
    shift_bins,
    reverse_flags,
    gain_one,
    bias_one,
    conv_weight,
    gain_two,
    bias_two,
    proj_weight,
    proj_bias,
    cotangent,
):
    seq_count, count_of_rows, channels = activations.shape
    reverse_mask = reverse_flags > 0
    moved = move_forward(
        activations, jnp.where(reverse_mask, -shift_bins, shift_bins), reverse_mask
    )
    moved_blocks = moved.reshape(MICRO, seq_count // MICRO, count_of_rows, channels)
    cot_blocks = cotangent.reshape(MICRO, seq_count // MICRO, count_of_rows, channels)
    piece_list = []
    for micro_index in range(MICRO):
        weights = gather_weights(
            gain_one, bias_one, conv_weight, gain_two, bias_two, proj_weight, proj_bias
        )
        piece_list.append(
            run_block(
                moved_blocks[micro_index : micro_index + 1],
                cot_blocks[micro_index : micro_index + 1],
                weights,
            )
        )
    output_blocks = jnp.concatenate([finished[0] for finished in piece_list], axis=0)
    grad_blocks = jnp.concatenate([finished[1] for finished in piece_list], axis=0)
    partials = piece_list[0][2]
    for finished in piece_list[1:]:
        partials = tuple((running + addend for running, addend in zip(partials, finished[2])))
    output = output_blocks.reshape(seq_count, count_of_rows, channels)
    grad_activations = move_backward(
        grad_blocks.reshape(seq_count, count_of_rows, channels), -shift_bins, reverse_mask
    )
    gain_one_sum, bias_one_sum, conv_sum, gain_two_sum, bias_two_sum, proj_sum, bias_sum = partials
    reduced = (
        lax.psum_scatter(conv_sum, ("dp", "bins"), scatter_dimension=1, tiled=True),
        lax.psum_scatter(proj_sum, ("dp", "bins"), scatter_dimension=1, tiled=True),
        lax.psum_scatter(bias_sum, ("dp", "bins"), scatter_dimension=0, tiled=True),
    )
    piece_wide = gain_one_sum.shape[0] // (lax.axis_size("dp") * lax.axis_size("bins"))
    start_wide = (
        lax.axis_index("dp") * lax.axis_size("bins") + lax.axis_index("bins")
    ) * piece_wide
    piece_narrow = gain_two_sum.shape[0] // lax.axis_size("bins")
    start_narrow = lax.axis_index("bins") * piece_narrow
    grad_gain_one = lax.dynamic_slice_in_dim(gain_one_sum, start_wide, piece_wide)
    grad_bias_one = lax.dynamic_slice_in_dim(bias_one_sum, start_wide, piece_wide)
    grad_gain_two = lax.dynamic_slice_in_dim(gain_two_sum, start_narrow, piece_narrow)
    grad_bias_two = lax.dynamic_slice_in_dim(bias_two_sum, start_narrow, piece_narrow)
    return (
        output,
        grad_activations,
        grad_gain_one,
        grad_bias_one,
        reduced[0],
        grad_gain_two,
        grad_bias_two,
        reduced[1],
        reduced[2],
    )


def solution(mesh):
    placed = (
        P("dp", "bins", None),
        P("dp"),
        P("dp"),
        P("bins"),
        P("bins"),
        P(None, "bins", None),
        P("bins"),
        P("bins"),
        P(None, "bins"),
        P("bins"),
        P("dp", "bins", None),
    )
    return jax.shard_map(
        local,
        mesh=mesh,
        in_specs=placed,
        out_specs=(
            P("dp", "bins", None),
            P("dp", "bins", None),
            P(("dp", "bins")),
            P(("dp", "bins")),
            P(None, ("dp", "bins"), None),
            P("bins"),
            P("bins"),
            P(None, ("dp", "bins")),
            P(("dp", "bins")),
        ),
        check_vma=False,
    )
```

profile of v0, /device:TPU:0, one launch (start us, length us, event | category | flops | bytes accessed | tf_op | source)
XLA Modules:
  0.0 852.2 jit_solution(6475871038135338338)
XLA Ops:
  7.2 3.8 copy.45
  11.6 5.3 collective-permute-done
  16.9 2.9 collective-permute-start.1
  19.8 68.5 %collective-permute-done.1 = bf16[16,128,768]{2,0,1:T(8,128)(2,1)} collective-permute-done((bf16[16,128,768]{2,0,1:T(8,128)(2,1)S(1)}, bf16[16,128,768]{2,0,1:T(8,128)(2,1)}, u32[]{:S(2)}, u32[]{:S(2)}) %collective-permute-start.1) | collective-permute-done | bytes 3145760 | tf_op jit(solution)/shard_map/ppermute | solution.py:18
  92.3 160.0 %all_gather.19 = bf16[384,768]{0,1:T(8,128)(2,1)} all-gather(bf16[384,96]{0,1:T(8,128)(2,1)S(1)} %copy-done.54), channel_id=1, replica_groups=mesh['dp'=4,'bins'=8] {'bins'}, dimensions={1}, use_global_device_ids=true | all-gather | bytes 663552 | tf_op jit(solution)/shard_map/all_gather | solution.py:79
  252.4 4.0 reverse_select_fusion.1
  259.4 3.7 collective-permute-start.3
  266.2 15.4 %all-reduce.13 = (bf16[768]{0:T(1024)(128)(2,1)}, bf16[768]{0:T(1024)(128)(2,1)S(1)}, bf16[768]{0:T(1024)(128)(2,1)S(1)}, bf16[384]{0:T(512)(128)(2,1)S(1)}, bf16[384]{0:T(512)(128)(2,1)S(1)}) all-reduce(bf16[768]{0:T(1024)(128)(2,1)S(1)} %dynamic-update-slice.4, ...), channel_id=1, replica_groups=mesh['dp'=4,'bins'=8] {'bins'}, use_global_device_ids=true, to_apply=%add.6 | all-reduce | flops 3072 | bytes 12288
  286.0 11.2 %gather_fusion = bf16[16,128,768]{2,0,1:T(8,128)(2,1)} fusion(bf16[16,134,768]{2,0,1:T(8,128)(2,1)S(1)} %pad_maximum_fusion, s32[16]{0:T(128)S(1)} %get-tuple-element.166), kind=kCustom, calls=%fused_computation | custom fusion | bytes 6291648 | tf_op jit(solution)/shard_map/vmap()/gather | solution.py:44
  297.2 4.0 fusion.274
  302.5 38.4 %all-reduce.12 = (f32[1,768]{1,0:T(1,128)S(1)}, f32[1,768]{1,0:T(1,128)S(1)}, f32[1,768]{1,0:T(1,128)S(1)}, f32[1,768]{1,0:T(1,128)S(1)}, f32[1,768]{1,0:T(1,128...) all-reduce(f32[1,768]{1,0:T(1,128)S(1)} %reduce_sum.455, ...), channel_id=1, replica_groups=mesh['dp'=4,'bins'=8] {'dp','bins'}, use_global_device_ids=true, to_apply=%region_3.4 | all-reduce | flops 6144 | bytes 49152 | tf_op jit(solution)/shard_map/psum | solution.py:98
  341.6 4.2 fusion.69
  347.9 3.0 collective-permute-start.11
  352.9 5.0 collective-permute-start.5
  364.9 4.3 collective-permute-start.7
  373.3 4.3 collective-permute-start.9
  384.7 40.7 %all-reduce.11 = (f32[1,384]{1,0:T(1,128)S(1)}, f32[1,384]{1,0:T(1,128)S(1)}, f32[1,384]{1,0:T(1,128)S(1)}, f32[1,384]{1,0:T(1,128)S(1)}, f32[1,384]{1,0:T(1,128...) all-reduce(f32[1,384]{1,0:T(1,128)S(1)} %reduce_sum.459, ...), channel_id=1, replica_groups=mesh['dp'=4,'bins'=8] {'dp','bins'}, use_global_device_ids=true, to_apply=%region_7.8 | all-reduce | flops 3072 | bytes 24576 | tf_op jit(solution)/shard_map/psum | solution.py:120
  425.7 3.4 fusion.268
  435.1 40.0 %all-reduce.10 = (f32[1,384]{1,0:T(1,128)S(1)}, f32[1,384]{1,0:T(1,128)S(1)}, f32[1,384]{1,0:T(1,128)S(1)}, f32[1,384]{1,0:T(1,128)S(1)}, f32[1,384]{1,0:T(1,128...) all-reduce(f32[1,384]{1,0:T(1,128)S(1)} %reduce_sum.511, ...), channel_id=1, replica_groups=mesh['dp'=4,'bins'=8] {'dp','bins'}, use_global_device_ids=true, to_apply=%region_59.60 | all-reduce | flops 3072 | bytes 24576 | tf_op jit(solution)/shard_map/psum | solution.py:142
  479.9 4.8 collective-permute-start.20
  486.3 4.3 collective-permute-start.16
  495.4 4.3 collective-permute-start.14
  516.0 44.4 %all-reduce.9 = (f32[1,768]{1,0:T(1,128)S(1)}, f32[1,768]{1,0:T(1,128)S(1)}, f32[1,768]{1,0:T(1,128)S(1)}, f32[1,768]{1,0:T(1,128)S(1)}, f32[1,768]{1,0:T(1,128)...) all-reduce(f32[1,768]{1,0:T(1,128)S(1)} %reduce_sum.515, ...), channel_id=1, replica_groups=mesh['dp'=4,'bins'=8] {'dp','bins'}, use_global_device_ids=true, to_apply=%region_63.64 | all-reduce | flops 6912 | bytes 55296 | tf_op jit(solution)/shard_map/psum | solution.py:183
  561.1 4.0 fusion.126
  567.3 3.4 copy.51
  590.7 66.0 %collective-permute-done.22 = bf16[16,128,768]{2,0,1:T(8,128)(2,1)} collective-permute-done((bf16[16,128,768]{2,0,1:T(8,128)(2,1)}, bf16[16,128,768]{2,0,1:T(8,128)(2,1)}, u32[]{:S(2)}, u32[]{:S(2)}) %collective-permute-start.22) | collective-permute-done | bytes 3145760 | tf_op jit(solution)/shard_map/ppermute | solution.py:18
  671.3 127.9 %collective-permute-done.23 = bf16[16,128,768]{2,0,1:T(8,128)(2,1)} collective-permute-done((bf16[16,128,768]{2,0,1:T(8,128)(2,1)}, bf16[16,128,768]{2,0,1:T(8,128)(2,1)}, u32[]{:S(2)}, u32[]{:S(2)}) %collective-permute-start.23) | collective-permute-done | bytes 3145760 | tf_op jit(solution)/shard_map/ppermute | solution.py:18
  799.2 3.9 reverse_select_fusion
  804.5 3.2 collective-permute-start.24
  809.5 11.2 %gather_fusion.1 = bf16[16,128,768]{2,0,1:T(8,128)(2,1)} fusion(bf16[16,134,768]{2,0,1:T(8,128)(2,1)S(1)} %pad_maximum_fusion.1, s32[16]{0:T(128)S(1)} %get-tuple-element.165), kind=kCustom, calls=%fused_computation.1 | custom fusion | bytes 6291648 | tf_op jit(solution)/shard_map/vmap()/gather | solution.py:44
  820.7 4.6 copy.69
  825.3 20.1 %reduce-scatter.5.cloned.1.call-done = f32[3,24,384]{2,1,0:T(8,128)} async-done(((f32[3,768,384]{2,1,0:T(8,128)}), f32[3,24,384]{2,1,0:T(8,128)}) %reduce-scatter.5.cloned.1.call-update) | async-done | bytes 110608 | tf_op jit(solution)/shard_map/reduce_scatter | solution.py:250
  (476 shorter events, 110.4 us)
Async XLA Ops:
  7.2 352.7 %all-gather.2.cloned.1.call-start = ((), (), s32[]{:S(2)}) async-start(), calls=%async_computation.2 | async-start | bytes 1990656 | tf_op jit(solution)/shard_map/all_gather | solution.py:76
  11.0 5.8 collective-permute-start
  16.9 71.4 %collective-permute-start.1 = (bf16[16,128,768]{2,0,1:T(8,128)(2,1)S(1)}, bf16[16,128,768]{2,0,1:T(8,128)(2,1)}, u32[]{:S(2)}, u32[]{:S(2)}) collective-permute-start(bf16[16,128,768]{2,0,1:T(8,128)(2,1)S(1)} %collective-permute-done), channel_id=1, source_target_pairs={{0,2},{1,3},{2,0},{3,1},{4,6},{5,7},{6,4},{7,5},{8,10},{9,11},{10,... | collective-permute-start | bytes 9437192 | tf_op jit(solution)/shard_map/ppermute | solution.py:18
  88.3 164.1 %collective-permute-start.2 = (bf16[16,128,768]{2,0,1:T(8,128)(2,1)}, bf16[16,128,768]{2,0,1:T(8,128)(2,1)}, u32[]{:S(2)}, u32[]{:S(2)}) collective-permute-start(bf16[16,128,768]{2,0,1:T(8,128)(2,1)} %collective-permute-done.1), channel_id=1, source_target_pairs={{0,4},{1,5},{2,6},{3,7},{4,0},{5,1},{6,2},{7,3},{8,12},{9,13},{10,... | collective-permute-start | bytes 9437192 | tf_op jit(solution)/shard_map/ppermute | solution.py:18
  91.1 734.2 %reduce-scatter.7.cloned.1.call-start = ((), (), s32[]{:S(2)}) async-start(), calls=%async_computation.4 | async-start | bytes 1216512
  91.2 161.2 %copy-start.26 = (bf16[16,128,768]{2,1,0:T(8,128)(2,1)S(1)}, bf16[16,128,768]{2,1,0:T(8,128)(2,1)}, u32[]{:S(2)}) copy-start(bf16[16,128,768]{2,1,0:T(8,128)(2,1)} %param.11) | copy-start | bytes 9437188
  91.7 164.7 %copy-start.126 = (pred[16]{0:T(512)(128)(4,1)}, pred[16]{0:T(512)(128)(4,1)S(1)}, u32[]{:S(2)}) copy-start(pred[16]{0:T(512)(128)(4,1)S(1)} %broadcast_compare_fusion) | copy-start | bytes 52
  258.1 25.2 %collective-permute-start.4 = (bf16[16,3,768]{2,0,1:T(8,128)(2,1)S(1)}, bf16[16,3,768]{2,0,1:T(8,128)(2,1)S(1)}, u32[]{:S(2)}, u32[]{:S(2)}) collective-permute-start(bf16[16,3,768]{2,0,1:T(8,128)(2,1)S(1)} %get-tuple-element.128), channel_id=1, source_target_pairs={{1,0},{2,1},{3,2},{4,3},{5,4},{6,5},{7,6},{9,8},{10,9},{11,10},{12... | collective-permute-start | bytes 221192 | tf_op jit(solution)/shard_map/ppermute | solution.py:29
  259.4 23.9 %collective-permute-start.3 = (bf16[16,3,768]{2,0,1:T(8,128)(2,1)S(1)}, bf16[16,3,768]{2,0,1:T(8,128)(2,1)}, u32[]{:S(2)}, u32[]{:S(2)}) collective-permute-start(bf16[16,3,768]{2,0,1:T(8,128)(2,1)S(1)} %get-tuple-element.127), channel_id=1, source_target_pairs={{0,1},{1,2},{2,3},{3,4},{4,5},{5,6},{6,7},{8,9},{9,10},{10,11},{11... | collective-permute-start | bytes 221192 | tf_op jit(solution)/shard_map/ppermute | solution.py:26
  346.6 35.9 %collective-permute-start.12 = (bf16[1,4,8,768]{3,2,1,0:T(8,128)(2,1)}, bf16[1,4,8,768]{3,2,1,0:T(8,128)(2,1)}, u32[]{:S(2)}, u32[]{:S(2)}) collective-permute-start(bf16[1,4,8,768]{3,2,1,0:T(8,128)(2,1)} %get-tuple-element.136), channel_id=1, source_target_pairs={{1,0},{2,1},{3,2},{4,3},{5,4},{6,5},{7,6},{9,8},{10,9},{11,10},{12... | collective-permute-start | bytes 147464 | tf_op jit(solution)/shard_map/ppermute | solution.py:29
  347.9 36.1 %collective-permute-start.11 = (bf16[1,4,8,768]{3,2,1,0:T(8,128)(2,1)S(1)}, bf16[1,4,8,768]{3,2,1,0:T(8,128)(2,1)S(1)}, u32[]{:S(2)}, u32[]{:S(2)}) collective-permute-start(bf16[1,4,8,768]{3,2,1,0:T(8,128)(2,1)S(1)} %get-tuple-element.135), channel_id=1, source_target_pairs={{0,1},{1,2},{2,3},{3,4},{4,5},{5,6},{6,7},{8,9},{9,10},{10,11},{11... | collective-permute-start | bytes 147464 | tf_op jit(solution)/shard_map/ppermute | solution.py:26
  351.6 13.1 %collective-permute-start.6 = (bf16[1,4,8,768]{3,2,1,0:T(8,128)(2,1)S(1)}, bf16[1,4,8,768]{3,2,1,0:T(8,128)(2,1)}, u32[]{:S(2)}, u32[]{:S(2)}) collective-permute-start(bf16[1,4,8,768]{3,2,1,0:T(8,128)(2,1)S(1)} %get-tuple-element.134), channel_id=1, source_target_pairs={{1,0},{2,1},{3,2},{4,3},{5,4},{6,5},{7,6},{9,8},{10,9},{11,10},{12... | collective-permute-start | bytes 147464 | tf_op jit(solution)/shard_map/ppermute | solution.py:29
  352.9 17.6 %collective-permute-start.5 = (bf16[1,4,8,768]{3,2,1,0:T(8,128)(2,1)}, bf16[1,4,8,768]{3,2,1,0:T(8,128)(2,1)S(1)}, u32[]{:S(2)}, u32[]{:S(2)}) collective-permute-start(bf16[1,4,8,768]{3,2,1,0:T(8,128)(2,1)} %get-tuple-element.133), channel_id=1, source_target_pairs={{0,1},{1,2},{2,3},{3,4},{4,5},{5,6},{6,7},{8,9},{9,10},{10,11},{11... | collective-permute-start | bytes 147464 | tf_op jit(solution)/shard_map/ppermute | solution.py:26
  358.6 14.7 %collective-permute-start.8 = (bf16[1,4,8,768]{3,2,1,0:T(8,128)(2,1)}, bf16[1,4,8,768]{3,2,1,0:T(8,128)(2,1)}, u32[]{:S(2)}, u32[]{:S(2)}) collective-permute-start(bf16[1,4,8,768]{3,2,1,0:T(8,128)(2,1)} %get-tuple-element.132), channel_id=1, source_target_pairs={{1,0},{2,1},{3,2},{4,3},{5,4},{6,5},{7,6},{9,8},{10,9},{11,10},{12... | collective-permute-start | bytes 147464 | tf_op jit(solution)/shard_map/ppermute | solution.py:29
  364.9 14.1 %collective-permute-start.7 = (bf16[1,4,8,768]{3,2,1,0:T(8,128)(2,1)S(1)}, bf16[1,4,8,768]{3,2,1,0:T(8,128)(2,1)S(1)}, u32[]{:S(2)}, u32[]{:S(2)}) collective-permute-start(bf16[1,4,8,768]{3,2,1,0:T(8,128)(2,1)S(1)} %copy-done.63), channel_id=1, source_target_pairs={{0,1},{1,2},{2,3},{3,4},{4,5},{5,6},{6,7},{8,9},{9,10},{10,11},{11... | collective-permute-start | bytes 147464 | tf_op jit(solution)/shard_map/ppermute | solution.py:26
  370.5 9.9 %collective-permute-start.10 = (bf16[1,4,8,768]{3,2,1,0:T(8,128)(2,1)S(1)}, bf16[1,4,8,768]{3,2,1,0:T(8,128)(2,1)S(1)}, u32[]{:S(2)}, u32[]{:S(2)}) collective-permute-start(bf16[1,4,8,768]{3,2,1,0:T(8,128)(2,1)S(1)} %get-tuple-element.130), channel_id=1, source_target_pairs={{1,0},{2,1},{3,2},{4,3},{5,4},{6,5},{7,6},{9,8},{10,9},{11,10},{12... | collective-permute-start | bytes 147464 | tf_op jit(solution)/shard_map/ppermute | solution.py:29
  373.3 7.7 collective-permute-start.9
  476.9 18.5 %collective-permute-start.18 = (bf16[1,4,8,384]{3,2,1,0:T(8,128)(2,1)S(1)}, bf16[1,4,8,384]{3,2,1,0:T(8,128)(2,1)S(1)}, u32[]{:S(2)}, u32[]{:S(2)}) collective-permute-start(bf16[1,4,8,384]{3,2,1,0:T(8,128)(2,1)S(1)} %get-tuple-element.141), channel_id=1, source_target_pairs={{0,1},{1,2},{2,3},{3,4},{4,5},{5,6},{6,7},{8,9},{9,10},{10,11},{11... | collective-permute-start | bytes 73736 | tf_op jit(solution)/shard_map/ppermute | solution.py:26
  478.3 15.0 %collective-permute-start.17 = (bf16[1,4,8,384]{3,2,1,0:T(8,128)(2,1)S(1)}, bf16[1,4,8,384]{3,2,1,0:T(8,128)(2,1)S(1)}, u32[]{:S(2)}, u32[]{:S(2)}) collective-permute-start(bf16[1,4,8,384]{3,2,1,0:T(8,128)(2,1)S(1)} %get-tuple-element.142), channel_id=1, source_target_pairs={{1,0},{2,1},{3,2},{4,3},{5,4},{6,5},{7,6},{9,8},{10,9},{11,10},{12... | collective-permute-start | bytes 73736 | tf_op jit(solution)/shard_map/ppermute | solution.py:29
  479.9 25.0 %collective-permute-start.20 = (bf16[1,4,8,384]{3,2,1,0:T(8,128)(2,1)S(1)}, bf16[1,4,8,384]{3,2,1,0:T(8,128)(2,1)S(1)}, u32[]{:S(2)}, u32[]{:S(2)}) collective-permute-start(bf16[1,4,8,384]{3,2,1,0:T(8,128)(2,1)S(1)} %get-tuple-element.143), channel_id=1, source_target_pairs={{0,1},{1,2},{2,3},{3,4},{4,5},{5,6},{6,7},{8,9},{9,10},{10,11},{11... | collective-permute-start | bytes 73736 | tf_op jit(solution)/shard_map/ppermute | solution.py:26
  484.7 17.9 %collective-permute-start.19 = (bf16[1,4,8,384]{3,2,1,0:T(8,128)(2,1)S(1)}, bf16[1,4,8,384]{3,2,1,0:T(8,128)(2,1)S(1)}, u32[]{:S(2)}, u32[]{:S(2)}) collective-permute-start(bf16[1,4,8,384]{3,2,1,0:T(8,128)(2,1)S(1)} %get-tuple-element.144), channel_id=1, source_target_pairs={{1,0},{2,1},{3,2},{4,3},{5,4},{6,5},{7,6},{9,8},{10,9},{11,10},{12... | collective-permute-start | bytes 73736 | tf_op jit(solution)/shard_map/ppermute | solution.py:29
  486.3 22.2 %collective-permute-start.16 = (bf16[1,4,8,384]{3,2,1,0:T(8,128)(2,1)S(1)}, bf16[1,4,8,384]{3,2,1,0:T(8,128)(2,1)S(1)}, u32[]{:S(2)}, u32[]{:S(2)}) collective-permute-start(bf16[1,4,8,384]{3,2,1,0:T(8,128)(2,1)S(1)} %get-tuple-element.139), channel_id=1, source_target_pairs={{0,1},{1,2},{2,3},{3,4},{4,5},{5,6},{6,7},{8,9},{9,10},{10,11},{11... | collective-permute-start | bytes 73736 | tf_op jit(solution)/shard_map/ppermute | solution.py:26
  493.4 14.5 %collective-permute-start.15 = (bf16[1,4,8,384]{3,2,1,0:T(8,128)(2,1)S(1)}, bf16[1,4,8,384]{3,2,1,0:T(8,128)(2,1)S(1)}, u32[]{:S(2)}, u32[]{:S(2)}) collective-permute-start(bf16[1,4,8,384]{3,2,1,0:T(8,128)(2,1)S(1)} %get-tuple-element.140), channel_id=1, source_target_pairs={{1,0},{2,1},{3,2},{4,3},{5,4},{6,5},{7,6},{9,8},{10,9},{11,10},{12... | collective-permute-start | bytes 73736 | tf_op jit(solution)/shard_map/ppermute | solution.py:29
  495.4 17.2 %collective-permute-start.14 = (bf16[1,4,8,384]{3,2,1,0:T(8,128)(2,1)S(1)}, bf16[1,4,8,384]{3,2,1,0:T(8,128)(2,1)S(1)}, u32[]{:S(2)}, u32[]{:S(2)}) collective-permute-start(bf16[1,4,8,384]{3,2,1,0:T(8,128)(2,1)S(1)} %get-tuple-element.137), channel_id=1, source_target_pairs={{0,1},{1,2},{2,3},{3,4},{4,5},{5,6},{6,7},{8,9},{9,10},{10,11},{11... | collective-permute-start | bytes 73736 | tf_op jit(solution)/shard_map/ppermute | solution.py:26
  502.7 9.3 %collective-permute-start.13 = (bf16[1,4,8,384]{3,2,1,0:T(8,128)(2,1)S(1)}, bf16[1,4,8,384]{3,2,1,0:T(8,128)(2,1)S(1)}, u32[]{:S(2)}, u32[]{:S(2)}) collective-permute-start(bf16[1,4,8,384]{3,2,1,0:T(8,128)(2,1)S(1)} %get-tuple-element.138), channel_id=1, source_target_pairs={{1,0},{2,1},{3,2},{4,3},{5,4},{6,5},{7,6},{9,8},{10,9},{11,10},{12... | collective-permute-start | bytes 73736 | tf_op jit(solution)/shard_map/ppermute | solution.py:29
  570.7 10.7 %collective-permute-start.21 = (bf16[16,128,768]{2,0,1:T(8,128)(2,1)}, bf16[16,128,768]{2,0,1:T(8,128)(2,1)}, u32[]{:S(2)}, u32[]{:S(2)}) collective-permute-start(bf16[16,128,768]{2,0,1:T(8,128)(2,1)} %copy.51), channel_id=1, source_target_pairs={{0,1},{1,0},{2,3},{3,2},{4,5},{5,4},{6,7},{7,6},{8,9},{9,8},{10,11... | collective-permute-start | bytes 9437192 | tf_op jit(solution)/shard_map/ppermute | solution.py:18
  576.0 269.4 %reduce-scatter.5.cloned.1.call-start = ((), (), s32[]{:S(2)}) async-start(), calls=%async_computation.3 | async-start | bytes 3649536 | tf_op jit(solution)/shard_map/reduce_scatter | solution.py:250
  581.4 75.3 %collective-permute-start.22 = (bf16[16,128,768]{2,0,1:T(8,128)(2,1)}, bf16[16,128,768]{2,0,1:T(8,128)(2,1)}, u32[]{:S(2)}, u32[]{:S(2)}) collective-permute-start(bf16[16,128,768]{2,0,1:T(8,128)(2,1)} %collective-permute-done.21), channel_id=1, source_target_pairs={{0,2},{1,3},{2,0},{3,1},{4,6},{5,7},{6,4},{7,5},{8,10},{9,11},{10,... | collective-permute-start | bytes 9437192 | tf_op jit(solution)/shard_map/ppermute | solution.py:18
  656.7 142.5 %collective-permute-start.23 = (bf16[16,128,768]{2,0,1:T(8,128)(2,1)}, bf16[16,128,768]{2,0,1:T(8,128)(2,1)}, u32[]{:S(2)}, u32[]{:S(2)}) collective-permute-start(bf16[16,128,768]{2,0,1:T(8,128)(2,1)} %collective-permute-done.22), channel_id=1, source_target_pairs={{0,4},{1,5},{2,6},{3,7},{4,0},{5,1},{6,2},{7,3},{8,12},{9,13},{10,... | collective-permute-start | bytes 9437192 | tf_op jit(solution)/shard_map/ppermute | solution.py:18
  666.9 132.4 %copy-start.127 = (pred[16]{0:T(512)(128)(4,1)S(1)}, pred[16]{0:T(512)(128)(4,1)}, u32[]{:S(2)}) copy-start(pred[16]{0:T(512)(128)(4,1)} %copy-done.126) | copy-start | bytes 52
  803.2 5.8 collective-permute-start.25
  804.5 4.6 collective-permute-start.24
  (136 other events, 1822.7 us)
Sparse Core Ops, SparseCore 0:
  91.2 93.1 all-gather.1
  576.1 160.0 reduce-scatter.6
  742.2 103.1 reduce-scatter.4
where the time goes:
time: 859 us; the launch traced here: 852 us
  blocking collectives  339 us (39%)
  waiting for transfers between devices  288 us (34%)
  starting transfers between devices  60.3 us (7%)
  matrix products  59.1 us (7%)
  local copies, waits for them, and re-layouts  51.6 us (6%)
  other arithmetic  36.7 us (4%)
  between operations  17.6 us (2%)
    ppermute x6, waiting for transfers between devices, partner(): return lax.ppermute(value, axis, pairs)  268 us
    all_gather x1, blocking collectives, gather_weights(): lax.all_gather(proj_weight, 'bins', axis=1, tiled=True)  160 us
    psum x1, blocking collectives, run_block(): lax.psum((jnp.sum(grad_normed_one, axis=(1, 2)), jnp.sum(grad_normed_one...  44.4 us
    psum x1, blocking collectives, run_block(): lax.psum((jnp.sum(conv_out, axis=(1, 2)), jnp.sum(conv_out * conv_out, ax...  40.7 us
    psum x1, blocking collectives, run_block(): lax.psum((jnp.sum(grad_normed_two, axis=(1, 2)), jnp.sum(grad_normed_two...  40 us
    psum x1, blocking collectives, run_block(): lax.psum((jnp.sum(inputs, axis=(1, 2)), jnp.sum(inputs * inputs, axis=(1,...  38.4 us
    ppermute x10, starting transfers between devices, with_halo(): lax.ppermute(lax.slice_in_dim(block, block.shape[dim] - width, None, axis...  38.2 us
    gather x2, local copies, waits for them, and re-layouts, shift_sequences(): lax.dynamic_slice_in_dim(sequence, starting_row, count_of_rows, 0)  22.4 us
  transfers between devices with their start and end apart: 29, of which 5 were waited for; matrix products, arithmetic and copies ran while one was open for 13% of the time, Pallas kernels for 0%

commit v1 on v0

v1 whole, which is shorter than its diff:
```python
import functools

import jax
import jax.numpy as jnp
from jax import lax
from jax.experimental import pallas as pl
from jax.experimental.pallas import tpu as pltpu
from jax.sharding import PartitionSpec as P

TAPS = 3
DILATION = 8
MICRO = 4
EPSILON = 1e-05
CHUNK = 32
BASE_SLOTS = 8
FIRST_SLOTS = 2
WINDOW = 2
EDGE = 16
VMEM_LIMIT = 60 * 1024 * 1024
MESH = pl.DeviceIdType.MESH
F32 = jnp.float32
BF16 = jnp.bfloat16
ROOT = 0.7978845608028654
CUBE = 0.044715


def vmem():
    return pl.BlockSpec(memory_space=pltpu.VMEM)


def smem():
    return pl.BlockSpec(memory_space=pltpu.SMEM)


def anywhere():
    return pl.BlockSpec(memory_space=pl.ANY)


def matmul(a, b, ca, cb):
    return lax.dot_general(a, b, (((ca,), (cb,)), ((), ())), preferred_element_type=F32)


class Place:
    def __init__(self, dp_count, bin_count):
        self.dp_count, self.bin_count = dp_count, bin_count
        self.chip_count = bin_count // 2
        self.dp = lax.axis_index("dp")
        self.bin = lax.axis_index("bins")
        self.chip = self.bin // 2
        self.core = lax.rem(self.bin, 2)

    def barrier(self):
        semaphore = pltpu.get_barrier_semaphore()
        for apart in range(1, self.bin_count):
            other = (self.dp, lax.rem(self.bin + apart, self.bin_count))
            pl.semaphore_signal(semaphore, inc=1, device_id=other, device_id_type=MESH)
        for apart in range(1, self.dp_count):
            for core in range(2):
                other = (lax.rem(self.dp + apart, self.dp_count), self.chip * 2 + core)
                pl.semaphore_signal(semaphore, inc=1, device_id=other, device_id_type=MESH)
        pl.semaphore_wait(semaphore, self.bin_count - 1 + 2 * (self.dp_count - 1))


def remote(source, target, sent, landed, device):
    return pltpu.make_async_remote_copy(
        src_ref=source,
        dst_ref=target,
        send_sem=sent,
        recv_sem=landed,
        device_id=device,
        device_id_type=MESH,
    )


class Stream:
    def __init__(self, place, source, target, sent, landed, count):
        self.source, self.target, self.sent, self.landed = source, target, sent, landed
        self.count, self.next = count, 0
        self.device = (place.dp, place.bin_count - 1 - place.bin)

    def piece(self, index):
        return remote(
            self.source.at[index],
            self.target.at[index],
            self.sent.at[index],
            self.landed.at[index],
            self.device,
        )

    def pump(self, pieces=1):
        for _ in range(pieces):
            if self.next >= self.count:
                return
            if self.next >= WINDOW:
                self.piece(self.next - WINDOW).wait_send()
            self.piece(self.next).start()
            self.next += 1

    def loop(self, trips, body, pieces):
        pieces = max(0, min(pieces, self.count - self.next, trips))
        if pieces == 0:
            lax.fori_loop(0, trips, lambda i, carry: (body(i), carry)[1], 0)
            return
        if self.next < WINDOW:
            self.pump(WINDOW - self.next)
            pieces = max(0, min(pieces, self.count - self.next))
        first = self.next
        every = trips // max(pieces, 1)

        def step(i, carry):
            body(i)
            done = lax.div(i, every)

            @pl.when((lax.rem(i, every) == 0) & (done < pieces))
            def _():
                self.piece(first + done - WINDOW).wait_send()
                self.piece(first + done).start()

            return carry

        lax.fori_loop(0, trips, step, 0)
        self.next = first + pieces

    def finish(self):
        self.pump(self.count)
        for index in range(max(0, self.count - WINDOW), self.count):
            self.piece(index).wait_send()
        for index in range(self.count):
            self.piece(index).wait_recv()


class AllReduce:
    def __init__(self, place, mine, near, far, near_sent, near_landed, far_sent, far_landed):
        self.place, self.mine, self.near, self.far = place, mine, near, far
        self.near_count = place.dp_count * 2
        self.me = place.dp * 2 + place.core
        self.near_copies = []
        for apart in range(1, self.near_count):
            to = lax.rem(self.me + apart, self.near_count)
            device = (to // 2, place.chip * 2 + lax.rem(to, 2))
            self.near_copies.append(
                remote(mine, near.at[apart - 1], near_sent.at[apart - 1], near_landed.at[apart - 1], device)
            )
        self.far_copies = []
        for apart in range(1, place.chip_count):
            to = lax.rem(place.chip + apart, place.chip_count)
            device = (place.dp, to * 2 + place.core)
            self.far_copies.append(
                remote(
                    near.at[self.near_count - 1],
                    far.at[apart - 1],
                    far_sent.at[apart - 1],
                    far_landed.at[apart - 1],
                    device,
                )
            )

    def start_near(self):
        for copy in self.near_copies:
            copy.start()

    def finish_near(self):
        for copy in self.near_copies:
            copy.wait()
        count = self.near_count

        total = None
        for member in range(count):
            apart = lax.rem(self.me - member + count, count)
            other = self.near[jnp.maximum(apart - 1, 0)]
            part = jnp.where(apart == 0, self.mine[...], other)
            total = part if total is None else total + part
        self.near[count - 1] = total

    def start_far(self):
        for copy in self.far_copies:
            copy.start()

    def finish_far(self):
        for copy in self.far_copies:
            copy.wait()
        count = self.place.chip_count
        total = None
        for member in range(count):
            apart = lax.rem(self.place.chip - member + count, count)
            part = jnp.where(
                apart == 0, self.near[self.near_count - 1], self.far[jnp.maximum(apart - 1, 0)]
            )
            total = part if total is None else total + part
        return total

    @staticmethod
    def scratch(dp_count, bin_count, rows, width):
        near, far = dp_count * 2, bin_count // 2
        return [
            pltpu.VMEM((rows, width), F32),
            pltpu.VMEM((near, rows, width), F32),
            pltpu.VMEM((far, rows, width), F32),
            pltpu.SemaphoreType.DMA((near,)),
            pltpu.SemaphoreType.DMA((near,)),
            pltpu.SemaphoreType.DMA((far,)),
            pltpu.SemaphoreType.DMA((far,)),
        ]


class Halo:
    def __init__(self, place, to_left, to_right, from_left, from_right, sent, landed):
        self.place, self.from_left, self.from_right = place, from_left, from_right
        count = place.bin_count
        self.right = remote(
            to_right, from_left, sent.at[0], landed.at[0], (place.dp, lax.rem(place.bin + 1, count))
        )
        self.left = remote(
            to_left, from_right, sent.at[1], landed.at[1], (place.dp, lax.rem(place.bin + count - 1, count))
        )
        self.first = place.bin == 0
        self.last = place.bin == count - 1

    def start(self):
        @pl.when(jnp.logical_not(self.last))
        def _():
            self.right.start()

        @pl.when(jnp.logical_not(self.first))
        def _():
            self.left.start()

        @pl.when(self.first)
        def _():
            self.from_left[...] = jnp.zeros_like(self.from_left)

        @pl.when(self.last)
        def _():
            self.from_right[...] = jnp.zeros_like(self.from_right)

    def finish(self):
        @pl.when(jnp.logical_not(self.last))
        def _():
            self.right.wait_send()
            self.left.wait_recv()

        @pl.when(jnp.logical_not(self.first))
        def _():
            self.left.wait_send()
            self.right.wait_recv()


def eighth(values):
    rows, width = values.shape
    return jnp.sum(values.reshape(rows // 8, 8, width), axis=0)


def first_kernel(dims, meta, x, x_edges, cot, shard, params, *rest):
    dp_count, bin_count, seqs, rows, chans, feats, base, first = dims
    (x_low, x_high, weights, totals, stage, extra, landed_cot) = rest[:7]
    (sums, own_stage) = rest[7:9]
    reduce_refs = rest[9:16]
    (halo_sent, halo_landed, one_sent, one_landed, two_sent, two_landed, three_sent, three_landed, local) = rest[16:25]
    cot_sent, cot_landed = rest[25:27]
    place = Place(dp_count, bin_count)
    per_slot = rows // CHUNK
    place.barrier()

    halo = Halo(
        place, x_edges.at[0], x_edges.at[1], x_low, x_high, halo_sent, halo_landed
    )
    halo.start()
    keep = pltpu.make_async_copy(
        shard.at[place.dp], weights.at[place.chip, place.core, place.dp], local.at[0]
    )
    keep.start()
    ones = []
    for apart in range(1, place.chip_count):
        to = lax.rem(place.chip + apart, place.chip_count)
        ones.append(
            remote(
                shard.at[place.dp],
                weights.at[place.chip, place.core, place.dp],
                one_sent.at[apart - 1],
                one_landed.at[apart - 1],
                (place.dp, to * 2 + place.core),
            )
        )
        ones[-1].start()

    def pack(target, slot, piece, origin):
        target[slot * per_slot + piece] = cot[meta[2, origin] * per_slot + piece]

    for slot in range(first):
        for piece in range(per_slot):
            pack(own_stage, slot, piece, slot)
    stream = Stream(place, own_stage, landed_cot, cot_sent, cot_landed, first * per_slot)

    sums[...] = jnp.zeros_like(sums)
    total_bins = rows * bin_count
    row = lax.broadcasted_iota(jnp.int32, (rows, 1), 0) + place.bin * rows

    def statistics(i):
        micro = i // (seqs // MICRO)
        target = row + meta[1, i]
        inside = jnp.where((target >= 0) & (target < total_bins), 1.0, 0.0).astype(F32)
        values = x[i].astype(F32) * inside
        sums[micro] += eighth(values)
        sums[MICRO + micro] += eighth(values * values)

    lax.fori_loop(0, seqs, lambda i, carry: (statistics(i), carry)[1], 0)
    mine = reduce_refs[0]
    mine[0 : 2 * MICRO] = jnp.sum(sums[...], axis=1)
    mine[2 * MICRO : 4 * MICRO] = params[...]
    reduce = AllReduce(place, *reduce_refs)
    reduce.start_near()
    stream.pump(2)

    for slot in range(first, base):
        for piece in range(per_slot):
            pack(stage, slot - first, piece, slot)
    for slot in range(base, seqs):
        for piece in range(per_slot):
            pack(extra, slot - base, piece, slot)

    keep.wait()
    for copy in ones:
        copy.wait()
    twos = []
    for apart in range(1, dp_count):
        to = lax.rem(place.dp + apart, dp_count)
        part = weights.at[:, place.core, place.dp]
        twos.append(
            remote(
                part, part, two_sent.at[apart - 1], two_landed.at[apart - 1], (to, place.bin)
            )
        )
        twos[-1].start()
    reduce.finish_near()
    reduce.start_far()
    stream.pump(2)
    totals[...] = reduce.finish_far()
    stream.pump(2)
    for copy in twos:
        copy.wait()
    half = weights.at[:, place.core]
    three = remote(half, half, three_sent.at[0], three_landed.at[0], (place.dp, place.bin + 1 - 2 * place.core))
    three.start()
    stream.pump(2)
    three.wait()
    halo.finish()
    stream.finish()


def run_first(dims, meta, x, x_edges, cot, shard, params):
    dp_count, bin_count, seqs, rows, chans, feats, base, first = dims
    per_slot = rows // CHUNK
    quarter = chans // bin_count // dp_count
    chips = bin_count // 2
    wshape = (chips, 2, dp_count, TAPS + 1, quarter, feats)
    dma = pltpu.SemaphoreType.DMA
    return pl.pallas_call(
        functools.partial(first_kernel, dims),
        out_shape=(
            jax.ShapeDtypeStruct((seqs, EDGE, chans), BF16),
            jax.ShapeDtypeStruct((seqs, EDGE, chans), BF16),
            jax.ShapeDtypeStruct(wshape, BF16),
            jax.ShapeDtypeStruct((4 * MICRO, chans), F32),
            jax.ShapeDtypeStruct(((base - first) * per_slot, CHUNK, chans), BF16),
            jax.ShapeDtypeStruct(((seqs - base) * per_slot, CHUNK, chans), BF16),
            jax.ShapeDtypeStruct((first * per_slot, CHUNK, chans), BF16),
        ),
        in_specs=[smem(), vmem(), anywhere(), vmem(), anywhere(), vmem()],
        out_specs=(vmem(), vmem(), anywhere(), vmem(), vmem(), vmem(), anywhere()),
        scratch_shapes=[
            pltpu.VMEM((2 * MICRO, 8, chans), F32),
            pltpu.VMEM((first * per_slot, CHUNK, chans), BF16),
            *AllReduce.scratch(dp_count, bin_count, 4 * MICRO, chans),
            dma((2,)),
            dma((2,)),
            dma((chips,)),
            dma((chips,)),
            dma((dp_count,)),
            dma((dp_count,)),
            dma((1,)),
            dma((1,)),
            dma((1,)),
            dma((first * per_slot,)),
            dma((first * per_slot,)),
        ],
        compiler_params=pltpu.CompilerParams(
            collective_id=0, has_side_effects=True, vmem_limit_bytes=VMEM_LIMIT
        ),
        name="first",
    )(meta, x, x_edges, cot, shard, params)


def norm_rows(totals, gains, count, scale_ref, offset_ref, inverse_ref, shift_ref):
    for micro in range(MICRO):
        mean = totals[micro : micro + 1] / count
        second = totals[MICRO + micro : MICRO + micro + 1] / count
        inverse = lax.rsqrt(second - mean * mean + EPSILON)
        scale = inverse * gains[0]
        scale_ref[micro] = scale
        offset_ref[micro] = gains[1] - mean * scale
        if inverse_ref is not None:
            inverse_ref[micro] = inverse
            shift_ref[micro] = -mean * inverse


def gelu(v):
    half = 0.5 * v
    return half + half * jnp.tanh(v * (ROOT + (ROOT * CUBE) * (v * v)))


def gelu_both(v):
    square = v * v
    half = 0.5 * v
    t = jnp.tanh(v * (ROOT + (ROOT * CUBE) * square))
    value = half + half * t
    slope = 0.5 + 0.5 * t + half * (1.0 - t * t) * (ROOT + (3.0 * ROOT * CUBE) * square)
    return value, slope


def forward_kernel(dims, meta, x, x_low, x_high, w, proj, totals, stage, *rest):
    dp_count, bin_count, seqs, rows, chans, feats, base, first = dims
    (moved, conv, out, out_stage, out_extra, landed_cot, totals_two) = rest[:7]
    (scale_one, offset_one, scale_two, offset_two, sums) = rest[7:12]
    reduce_refs = rest[12:19]
    cot_sent, cot_landed = rest[19:21]
    place = Place(dp_count, bin_count)
    per_slot = rows // CHUNK
    pieces = (base - first) * per_slot
    place.barrier()
    stream = Stream(place, stage, landed_cot, cot_sent, cot_landed, pieces)
    stream.pump(WINDOW)
    per_micro = seqs // MICRO
    count = float(per_micro * rows * dp_count * bin_count)
    stats = totals[...]
    params = stats[2 * MICRO :]
    norm_rows(stats, (params[0:1], params[1:2]), count, scale_one, offset_one, None, None)
    proj_bias = params[2:3]
    sums[...] = jnp.zeros_like(sums)

    long_rows = rows + 2 * DILATION
    across = rows + 2 * EDGE
    local_row = lax.broadcasted_iota(jnp.int32, (long_rows, across), 0) - DILATION
    column = lax.broadcasted_iota(jnp.int32, (long_rows, across), 1)
    mask_row = lax.broadcasted_iota(jnp.int32, (long_rows, 1), 0) - DILATION
    total_bins = rows * bin_count

    def up(i):
        micro = i // per_micro
        reverse, shift = meta[0, i], meta[1, i]
        direction = 1 - 2 * reverse
        begin = reverse * (rows - 1)
        pick = jnp.where(column == local_row * direction + (begin - shift + EDGE), 1.0, 0.0).astype(BF16)
        source = jnp.concatenate([x_low[i], x[i], x_high[i]], axis=0)
        shifted = matmul(pick, source, 1, 0)
        moved[i] = shifted[DILATION : DILATION + rows].astype(BF16)
        hidden = gelu(shifted * scale_one[micro] + offset_one[micro])
        where = place.bin * rows + begin + mask_row * direction
        hidden = jnp.where((where >= 0) & (where < total_bins), hidden, 0.0)
        result = None
        for tap in range(TAPS):
            window = hidden[tap * DILATION : tap * DILATION + rows].astype(BF16)
            term = matmul(window, w[tap], 1, 0)
            result = term if result is None else result + term
        conv[i] = result
        sums[micro] += eighth(result)
        sums[MICRO + micro] += eighth(result * result)

    stream.loop(seqs, up, seqs)
    mine = reduce_refs[0]
    mine[...] = jnp.sum(sums[...], axis=1)
    reduce = AllReduce(place, *reduce_refs)
    reduce.start_near()
    stream.pump(1)
    reduce.finish_near()
    reduce.start_far()
    stream.pump(2)
    stats_two = reduce.finish_far()
    totals_two[...] = stats_two
    norm_rows(
        stats_two, (params[3:4, :feats], params[3:4, feats : 2 * feats]), count, scale_two, offset_two, None, None
    )

    def down(i):
        micro = i // per_micro
        hidden = gelu(conv[i] * scale_two[micro] + offset_two[micro]).astype(BF16)
        branch = matmul(hidden, proj[...], 1, 1) + proj_bias
        out[i] = (moved[i].astype(F32) + branch).astype(BF16)

    stream.loop(seqs, down, seqs)
    for slot in range(base):
        origin = meta[2, slot]
        for piece in range(per_slot):
            out_stage[slot * per_slot + piece] = out[origin, piece * CHUNK : (piece + 1) * CHUNK]
    for slot in range(base, seqs):
        origin = meta[2, slot]
        for piece in range(per_slot):
            out_extra[(slot - base) * per_slot + piece] = out[origin, piece * CHUNK : (piece + 1) * CHUNK]
    stream.finish()


def run_forward(dims, meta, x, x_low, x_high, w, proj, totals, stage):
    dp_count, bin_count, seqs, rows, chans, feats, base, first = dims
    per_slot = rows // CHUNK
    pieces = (base - first) * per_slot
    dma = pltpu.SemaphoreType.DMA
    return pl.pallas_call(
        functools.partial(forward_kernel, dims),
        out_shape=(
            jax.ShapeDtypeStruct((seqs, rows, chans), BF16),
            jax.ShapeDtypeStruct((seqs, rows, feats), F32),
            jax.ShapeDtypeStruct((seqs, rows, chans), BF16),
            jax.ShapeDtypeStruct((base * per_slot, CHUNK, chans), BF16),
            jax.ShapeDtypeStruct(((seqs - base) * per_slot, CHUNK, chans), BF16),
            jax.ShapeDtypeStruct((pieces, CHUNK, chans), BF16),
            jax.ShapeDtypeStruct((2 * MICRO, feats), F32),
        ),
        in_specs=[smem(), *[vmem()] * 6, anywhere()],
        out_specs=(*[vmem()] * 5, anywhere(), vmem()),
        scratch_shapes=[
            pltpu.VMEM((MICRO, 1, chans), F32),
            pltpu.VMEM((MICRO, 1, chans), F32),
            pltpu.VMEM((MICRO, 1, feats), F32),
            pltpu.VMEM((MICRO, 1, feats), F32),
            pltpu.VMEM((2 * MICRO, 8, feats), F32),
            *AllReduce.scratch(dp_count, bin_count, 2 * MICRO, feats),
            dma((pieces,)),
            dma((pieces,)),
        ],
        compiler_params=pltpu.CompilerParams(
            collective_id=1, has_side_effects=True, vmem_limit_bytes=VMEM_LIMIT
        ),
        name="forward",
    )(meta, x, x_low, x_high, w, proj, totals, stage)


def backward_kernel(dims, meta, moved, conv, w, proj, totals, totals_two, cot, cot_a, cot_b, cot_c, out_stage, *rest):
    dp_count, bin_count, seqs, rows, chans, feats, base, first = dims
    (grads, low_edge, high_edge, landed_out, sums_two_out, sums_one_out, partial) = rest[:7]
    (cots, scale_one, offset_one, inverse_one, shift_one) = rest[7:12]
    (scale_two, offset_two, inverse_two, shift_two) = rest[12:16]
    (grad_two, grad_one, hidden_all, cotangents_unused, conv_grad, hidden_group, window_group) = rest[16:23]
    (sums_two, sums_one, bias_sum, const_two, const_one) = rest[23:28]
    (send_left, send_right, from_left, from_right, last_left, last_right, last_from_left, last_from_right) = rest[28:36]
    reduce_two = rest[36:43]
    reduce_one = rest[43:50]
    (local, halo_sent, halo_landed, last_sent, last_landed, out_sent, out_landed) = rest[50:57]
    place = Place(dp_count, bin_count)
    per_slot = rows // CHUNK
    per_micro = seqs // MICRO
    loads = [
        pltpu.make_async_copy(cot, cots.at[0:seqs], local.at[0]),
        pltpu.make_async_copy(cot_a, cots.at[seqs : seqs + first], local.at[1]),
        pltpu.make_async_copy(cot_b, cots.at[seqs + first : seqs + base], local.at[2]),
        pltpu.make_async_copy(cot_c, cots.at[seqs + base : 2 * seqs], local.at[3]),
    ]
    for load in loads:
        load.start()
    place.barrier()
    stream = Stream(place, out_stage, landed_out, out_sent, out_landed, base * per_slot)
    stream.pump(WINDOW)
    count = float(per_micro * rows * dp_count * bin_count)
    stats = totals[...]
    params = stats[2 * MICRO :]
    stats_two = totals_two[...]
    norm_rows(stats, (params[0:1], params[1:2]), count, scale_one, offset_one, inverse_one, shift_one)
    norm_rows(
        stats_two,
        (params[3:4, :feats], params[3:4, feats : 2 * feats]),
        count,
        scale_two,
        offset_two,
        inverse_two,
        shift_two,
    )
    sums_two[...] = jnp.zeros_like(sums_two)
    sums_one[...] = jnp.zeros_like(sums_one)
    bias_sum[...] = jnp.zeros_like(bias_sum)
    partial[...] = jnp.zeros_like(partial)
    for load in loads:
        load.wait()

    def head(i):
        micro = i // per_micro
        cotangent = cots[meta[3, i]]
        bias_sum[...] += eighth(cotangent.astype(F32))
        values = conv[i]
        hidden, slope = gelu_both(values * scale_two[micro] + offset_two[micro])
        hidden_all[i] = hidden.astype(BF16)
        grad = matmul(cotangent, proj[...], 1, 0) * slope
        grad_two[i] = grad
        centred = values * inverse_two[micro] + shift_two[micro]
        sums_two[micro] += eighth(grad)
        sums_two[MICRO + micro] += eighth(grad * centred)
        partial[TAPS] += matmul(cotangent, hidden_all[i], 0, 0)

    stream.loop(seqs, head, seqs // 2)
    mine = reduce_two[0]
    mine[0 : 2 * MICRO] = jnp.sum(sums_two[...], axis=1)
    bias_row = jnp.sum(bias_sum[...], axis=0, keepdims=True)
    spare = jnp.zeros((1, feats), F32)
    for part in range(2 * MICRO):
        begin = part * feats
        mine[2 * MICRO + part : 2 * MICRO + part + 1] = bias_row[:, begin : begin + feats] if begin < chans else spare
    reduce = AllReduce(place, *reduce_two)
    reduce.start_near()
    stream.pump(1)
    reduce.finish_near()
    reduce.start_far()
    stream.pump(2)
    back_two = reduce.finish_far()
    sums_two_out[...] = back_two
    for micro in range(MICRO):
        const_two[micro] = back_two[micro : micro + 1] / count
        const_two[MICRO + micro] = back_two[MICRO + micro : MICRO + micro + 1] / count

    def middle(i):
        micro = i // per_micro
        reverse = meta[0, i]
        centred = conv[i] * inverse_two[micro] + shift_two[micro]
        value = scale_two[micro] * (grad_two[i] - const_two[micro] - centred * const_two[MICRO + micro])
        value = value.astype(BF16).astype(F32)
        conv_grad[i] = value
        top, bottom = value[:DILATION], value[rows - DILATION :]
        send_left[i] = jnp.where(reverse > 0, bottom, top)
        send_right[i] = jnp.where(reverse > 0, top, bottom)

    lax.fori_loop(0, seqs, lambda i, carry: (middle(i), carry)[1], 0)
    halo = Halo(place, send_left, send_right, from_left, from_right, halo_sent, halo_landed)
    halo.start()
    stream.pump(2)
    halo.finish()

    def tail(i):
        micro = i // per_micro
        inner = lax.rem(i, per_micro)
        reverse = meta[0, i]
        left, right = from_left[i], from_right[i]
        low = jnp.where(reverse > 0, right, left)
        high = jnp.where(reverse > 0, left, right)
        full = jnp.concatenate([low, conv_grad[i], high], axis=0)
        grad = None
        for tap in range(TAPS):
            begin = (TAPS - 1 - tap) * DILATION
            window = full[begin : begin + rows].astype(BF16)
            window_group[tap, pl.ds(pl.multiple_of(inner * rows, rows), rows)] = window
            term = matmul(window, w[tap], 1, 1)
            grad = term if grad is None else grad + term
        values = moved[i].astype(F32)
        hidden, slope = gelu_both(values * scale_one[micro] + offset_one[micro])
        hidden_group[pl.ds(pl.multiple_of(inner * rows, rows), rows)] = hidden.astype(BF16)
        grad = grad * slope
        grad_one[i] = grad
        centred = values * inverse_one[micro] + shift_one[micro]
        sums_one[micro] += eighth(grad)
        sums_one[MICRO + micro] += eighth(grad * centred)

    for micro in range(MICRO):

        def one(inner, carry, micro=micro):
            tail(micro * per_micro + inner)
            return carry

        stream.loop(per_micro, lambda inner, micro=micro: tail(micro * per_micro + inner), per_micro // 2)
        for tap in range(TAPS):
            partial[tap] += matmul(hidden_group[...], window_group[tap], 0, 0)

    mine = reduce_one[0]
    mine[...] = jnp.sum(sums_one[...], axis=1)
    reduce = AllReduce(place, *reduce_one)
    reduce.start_near()
    stream.pump(1)
    reduce.finish_near()
    reduce.start_far()
    stream.pump(2)
    back_one = reduce.finish_far()
    sums_one_out[...] = back_one
    for micro in range(MICRO):
        const_one[micro] = back_one[micro : micro + 1] / count
        const_one[MICRO + micro] = back_one[MICRO + micro : MICRO + micro + 1] / count

    def end(i):
        micro = i // per_micro
        reverse = meta[0, i]
        centred = moved[i].astype(F32) * inverse_one[micro] + shift_one[micro]
        value = grad_one[i] - const_one[micro] - centred * const_one[MICRO + micro]
        value = cots[meta[3, i]].astype(F32) + scale_one[micro] * value
        grads[i] = value.astype(BF16)
        top, bottom = value[:EDGE].astype(BF16), value[rows - EDGE :].astype(BF16)
        last_left[i] = jnp.where(reverse > 0, bottom, top)
        last_right[i] = jnp.where(reverse > 0, top, bottom)

    stream.loop(seqs, end, seqs // 4)
    last = Halo(place, last_left, last_right, last_from_left, last_from_right, last_sent, last_landed)
    last.start()
    stream.pump(2)
    last.finish()
    low_edge[...] = last_from_left[...]
    high_edge[...] = last_from_right[...]
    stream.finish()


def run_backward(dims, meta, moved, conv, w, proj, totals, totals_two, cot, cot_a, cot_b, cot_c, out_stage):
    dp_count, bin_count, seqs, rows, chans, feats, base, first = dims
    per_slot = rows // CHUNK
    per_micro = seqs // MICRO
    dma = pltpu.SemaphoreType.DMA
    wide = pltpu.VMEM((MICRO, 1, chans), F32)
    narrow = pltpu.VMEM((MICRO, 1, feats), F32)
    return pl.pallas_call(
        functools.partial(backward_kernel, dims),
        out_shape=(
            jax.ShapeDtypeStruct((seqs, rows, chans), BF16),
            jax.ShapeDtypeStruct((seqs, EDGE, chans), BF16),
            jax.ShapeDtypeStruct((seqs, EDGE, chans), BF16),
            jax.ShapeDtypeStruct((base * per_slot, CHUNK, chans), BF16),
            jax.ShapeDtypeStruct((4 * MICRO, feats), F32),
            jax.ShapeDtypeStruct((2 * MICRO, chans), F32),
            jax.ShapeDtypeStruct((TAPS + 1, chans, feats), F32),
        ),
        in_specs=[smem(), *[vmem()] * 6, *[anywhere()] * 5],
        out_specs=(vmem(), vmem(), vmem(), anywhere(), vmem(), vmem(), vmem()),
        scratch_shapes=[
            pltpu.VMEM((2 * seqs, rows, chans), BF16),
            wide,
            wide,
            wide,
            wide,
            narrow,
            narrow,
            narrow,
            narrow,
            pltpu.VMEM((seqs, rows, feats), F32),
            pltpu.VMEM((seqs, rows, chans), F32),
            pltpu.VMEM((seqs, rows, feats), BF16),
            pltpu.VMEM((8, 128), F32),
            pltpu.VMEM((seqs, rows, feats), F32),
            pltpu.VMEM((per_micro * rows, chans), BF16),
            pltpu.VMEM((TAPS, per_micro * rows, feats), BF16),
            pltpu.VMEM((2 * MICRO, 8, feats), F32),
            pltpu.VMEM((2 * MICRO, 8, chans), F32),
            pltpu.VMEM((8, chans), F32),
            pltpu.VMEM((2 * MICRO, 1, feats), F32),
            pltpu.VMEM((2 * MICRO, 1, chans), F32),
            *[pltpu.VMEM((seqs, DILATION, feats), F32)] * 4,
            *[pltpu.VMEM((seqs, EDGE, chans), BF16)] * 4,
            *AllReduce.scratch(dp_count, bin_count, 4 * MICRO, feats),
            *AllReduce.scratch(dp_count, bin_count, 2 * MICRO, chans),
            dma((4,)),
            dma((2,)),
            dma((2,)),
            dma((2,)),
            dma((2,)),
            dma((base * per_slot,)),
            dma((base * per_slot,)),
        ],
        compiler_params=pltpu.CompilerParams(
            collective_id=2, has_side_effects=True, vmem_limit_bytes=VMEM_LIMIT
        ),
        name="backward",
    )(meta, moved, conv, w, proj, totals, totals_two, cot, cot_a, cot_b, cot_c, out_stage)


def last_kernel(rows, meta, grad, left, right, out, near, far, result_out, result_grad):
    i = pl.program_id(0)
    reverse, shift, slot, near_slots = meta[0, i], meta[1, i], meta[4, i], meta[5, i]
    crossed = jnp.where(slot < near_slots, near[0], far[0])
    result_out[0] = jnp.where(reverse > 0, crossed, out[0])
    low = jnp.where(reverse > 0, right[0], left[0])
    high = jnp.where(reverse > 0, left[0], right[0])
    source = jnp.concatenate([low, grad[0], high], axis=0)
    across = rows + 2 * EDGE
    row = lax.broadcasted_iota(jnp.int32, (rows, across), 0)
    column = lax.broadcasted_iota(jnp.int32, (rows, across), 1)
    place = jnp.where(reverse > 0, rows - 1 - row - shift, row + shift) + EDGE
    pick = jnp.where(column == place, 1.0, 0.0).astype(BF16)
    result_grad[0] = matmul(pick, source, 1, 0).astype(BF16)


def run_last(dims, meta, grad, left, right, out, near, far):
    dp_count, bin_count, seqs, rows, chans, feats, base, first = dims
    full = (1, rows, chans)
    edge = (1, EDGE, chans)
    own = lambda i, meta: (i, 0, 0)
    return pl.pallas_call(
        functools.partial(last_kernel, rows),
        out_shape=(
            jax.ShapeDtypeStruct((seqs, rows, chans), BF16),
            jax.ShapeDtypeStruct((seqs, rows, chans), BF16),
        ),
        grid_spec=pltpu.PrefetchScalarGridSpec(
            num_scalar_prefetch=1,
            grid=(seqs,),
            in_specs=[
                pl.BlockSpec(full, own),
                pl.BlockSpec(edge, own),
                pl.BlockSpec(edge, own),
                pl.BlockSpec(full, own),
                pl.BlockSpec(full, lambda i, meta: (jnp.minimum(meta[4, i], base - 1), 0, 0)),
                pl.BlockSpec(full, lambda i, meta: (jnp.maximum(meta[4, i] - base, 0), 0, 0)),
            ],
            out_specs=(pl.BlockSpec(full, own), pl.BlockSpec(full, own)),
        ),
        name="last",
    )(meta, grad, left, right, out, near, far)


def local(
    activations,
    shift_bins,
    reverse_flags,
    gain_one,
    bias_one,
    conv_weight,
    gain_two,
    bias_two,
    proj_weight,
    proj_bias,
    cotangent,
):
    seqs, rows, chans = activations.shape
    feats = conv_weight.shape[2]
    dp_count, bin_count = lax.axis_size("dp"), lax.axis_size("bins")
    dp, bins = lax.axis_index("dp"), lax.axis_index("bins")
    per_slot = rows // CHUNK
    base, first = BASE_SLOTS, FIRST_SLOTS
    dims = (dp_count, bin_count, seqs, rows, chans, feats, base, first)

    reverse = (reverse_flags > 0).astype(jnp.int32)
    index = jnp.arange(seqs, dtype=jnp.int32)
    before = jnp.sum(jnp.where(index[None, :] < index[:, None], reverse[None, :], 0), axis=1)
    slot = jnp.where(reverse > 0, before, 0)
    origin = jnp.sum(
        jnp.where((slot[None, :] == index[:, None]) & (reverse[None, :] > 0), index[None, :], 0), axis=1
    )
    chosen = jnp.where(reverse > 0, seqs + slot, index)
    meta = jnp.stack([reverse, shift_bins, origin, chosen, slot, jnp.full((seqs,), base, jnp.int32)])
    reversed_count = jnp.sum(reverse)

    lane = jnp.arange(chans, dtype=jnp.int32)
    at_home = dp == 0

    def spread(vector):
        size = vector.shape[0]
        width = size * bin_count
        held = jnp.tile(vector.astype(F32), bin_count)
        return jnp.where((jnp.arange(width) // size == bins) & at_home, held, 0.0)

    counts = jnp.where((lane == dp) & (bins == 0), reversed_count.astype(F32), 0.0)
    nothing = jnp.zeros((chans,), F32)
    params = jnp.stack(
        [
            spread(gain_one),
            spread(bias_one),
            spread(proj_bias),
            jnp.concatenate([spread(gain_two), spread(bias_two)]),
            counts,
            nothing,
            nothing,
            nothing,
        ]
    )
    share = chans // bin_count
    quarter = share // dp_count
    shard = jnp.concatenate([conv_weight, proj_weight.T[None]], axis=0)
    shard = shard.reshape(TAPS + 1, dp_count, quarter, feats).transpose(1, 0, 2, 3)
    edges = jnp.stack([activations[:, :EDGE], activations[:, rows - EDGE :]])

    x_low, x_high, weights, totals, stage, cot_extra, cot_a = run_first(
        dims, meta, activations, edges, cotangent.reshape(seqs * per_slot, CHUNK, chans), shard, params
    )
    full = weights.transpose(3, 0, 1, 2, 4, 5).reshape(TAPS + 1, chans, feats)
    w, proj = full[:TAPS], full[TAPS]
    most = jnp.max(totals[3 * MICRO, :dp_count]).astype(jnp.int32)

    moved, conv, out, out_stage, out_extra, cot_b, totals_two = run_forward(
        dims, meta, activations, x_low, x_high, w, proj, totals, stage
    )

    pairs = [(source, bin_count - 1 - source) for source in range(bin_count)]

    def crossing(slots, pair):
        if slots == 0:
            return pair
        held = slots * per_slot
        got = lax.ppermute(jnp.concatenate([item[:held] for item in pair]), "bins", pairs)
        return tuple(
            lax.dynamic_update_slice_in_dim(item, got[k * held : (k + 1) * held], 0, 0)
            for k, item in enumerate(pair)
        )

    extra = lax.switch(
        jnp.clip(most - base, 0, seqs - base),
        [functools.partial(crossing, slots) for slots in range(seqs - base + 1)],
        (cot_extra, out_extra),
    )

    slots_of = lambda item: item.reshape(-1, rows, chans)
    grads, low_edge, high_edge, out_near, back_two, back_one, partial = run_backward(
        dims,
        meta,
        moved,
        conv,
        w,
        proj,
        totals,
        totals_two,
        cotangent,
        slots_of(cot_a),
        slots_of(cot_b),
        slots_of(extra[0]),
        out_stage,
    )
    output, grad_activations = run_last(
        dims, meta, grads, low_edge, high_edge, out, slots_of(out_near), slots_of(extra[1])
    )

    scattered = lax.psum_scatter(partial, ("dp", "bins"), scatter_dimension=1, tiled=True)
    wide = chans // (dp_count * bin_count)
    narrow = feats // bin_count
    wide_at = (dp * bin_count + bins) * wide
    narrow_at = bins * narrow
    bias_sum = back_two[2 * MICRO :].reshape(-1)[:chans]
    cut = lax.dynamic_slice_in_dim
    return (
        output,
        grad_activations,
        cut(jnp.sum(back_one[MICRO:], axis=0), wide_at, wide),
        cut(jnp.sum(back_one[:MICRO], axis=0), wide_at, wide),
        scattered[:TAPS],
        cut(jnp.sum(back_two[MICRO : 2 * MICRO], axis=0), narrow_at, narrow),
        cut(jnp.sum(back_two[:MICRO], axis=0), narrow_at, narrow),
        scattered[TAPS].T,
        cut(bias_sum, wide_at, wide),
    )


def solution(mesh):
    placed = (
        P("dp", "bins", None),
        P("dp"),
        P("dp"),
        P("bins"),
        P("bins"),
        P(None, "bins", None),
        P("bins"),
        P("bins"),
        P(None, "bins"),
        P("bins"),
        P("dp", "bins", None),
    )
    return jax.shard_map(
        local,
        mesh=mesh,
        in_specs=placed,
        out_specs=(
            P("dp", "bins", None),
            P("dp", "bins", None),
            P(("dp", "bins")),
            P(("dp", "bins")),
            P(None, ("dp", "bins"), None),
            P("bins"),
            P("bins"),
            P(None, ("dp", "bins")),
            P(("dp", "bins")),
        ),
        check_vma=False,
    )
```

time: 859 us -> 397 us (0.46); the launches traced: 852 us -> 404 us
  blocking collectives: 339 us -> 0 us
  Pallas kernels: 0 us -> 234 us
  waiting for transfers between devices: 288 us -> 125 us
  matrix products: 59.1 us -> 0 us
  starting transfers between devices: 60.3 us -> 2.83 us
  other arithmetic: 36.7 us -> 5.42 us
  local copies, waits for them, and re-layouts: 51.6 us -> 20.6 us
    ppermute x26 -> x1, waiting for transfers between devices: 268 us -> 26.2 us  [crossing(): lax.ppermute(jnp.concatenate([item[:held] for item in pair]), 'bins', pairs)]
    pallas_call x0 -> x4, Pallas kernels: none -> 234 us  [the longest x1 111 us: run_backward(): pl.pallas_call(functools.partial(backward_kernel, dims), out_shape=(jax.S...]
    psum x4 -> x0, blocking collectives: 163 us -> none  [the longest x1 44.4 us: run_block(): lax.psum((jnp.sum(grad_normed_one, axis=(1, 2)), jnp.sum(grad_normed_one...]
    all_gather x1 -> x0, blocking collectives: 160 us -> none  [gather_weights(): lax.all_gather(proj_weight, 'bins', axis=1, tiled=True)]
    reduce_scatter x1, waiting for transfers between devices: 20.1 us -> 99.2 us  [local(): lax.psum_scatter(partial, ('dp', 'bins'), scatter_dimension=1, tiled=True)]
    dot_general x48 -> x0, matrix products: 59.1 us -> none  [the longest x12 16.4 us: run_block(): jnp.einsum('mblf,cf->mblc', sliding_window, conv_weight[kernel_tap_index]...]
    ppermute x26 -> x1, starting transfers between devices: 60 us -> 2.79 us  [crossing(): lax.ppermute(jnp.concatenate([item[:held] for item in pair]), 'bins', pairs)]
    gather x2 -> x0, local copies, waits for them, and re-layouts: 22.4 us -> none  [shift_sequences(): lax.dynamic_slice_in_dim(sequence, starting_row, count_of_rows, 0)]
  transfers between devices with their start and end apart: 29 -> 2, of which waited for: 5 -> 2; matrix products, arithmetic and copies ran while one was open for 13% -> 1% of each run, Pallas kernels for 0% -> 3%
where the time goes in v1:
time: 397 us; the launch traced here: 404 us
  Pallas kernels  234 us (59%)
  waiting for transfers between devices  125 us (31%)
  local copies, waits for them, and re-layouts  20.6 us (5%)
  between operations  15.5 us (4%)
  other arithmetic  5.42 us (1%)
    pallas_call x1, Pallas kernels, run_backward(): pl.pallas_call(functools.partial(backward_kernel, dims), out_shape=(jax.S...  111 us
    reduce_scatter x1, waiting for transfers between devices, local(): lax.psum_scatter(partial, ('dp', 'bins'), scatter_dimension=1, tiled=True)  99.2 us
    pallas_call x1, Pallas kernels, run_forward(): pl.pallas_call(functools.partial(forward_kernel, dims), out_shape=(jax.Sh...  69 us
    pallas_call x1, Pallas kernels, run_first(): pl.pallas_call(functools.partial(first_kernel, dims), out_shape=(jax.Shap...  41 us
    ppermute x1, waiting for transfers between devices, crossing(): lax.ppermute(jnp.concatenate([item[:held] for item in pair]), 'bins', pairs)  26.2 us
    pallas_call x1, Pallas kernels, run_last(): pl.pallas_call(functools.partial(last_kernel, rows), out_shape=(jax.Shape...  13.3 us
  transfers between devices with their start and end apart: 2, of which 2 were waited for; matrix products, arithmetic and copies ran while one was open for 1% of the time, Pallas kernels for 3%

profile of v1, /device:TPU:0, one launch (start us, length us, event | category | flops | bytes accessed | tf_op | source)
XLA Modules:
  0.0 404.2 jit_solution(12352159492191181862)
XLA Ops:
  7.3 0.7 broadcast_compare_fusion
  8.1 1.3 select_bitcast_fusion
  10.0 0.7 tile.20
  10.8 0.7 tile.22
  11.5 0.7 tile.51
  12.3 0.7 tile.53
  13.0 0.7 tile.24
  13.8 1.2 slice_bitcast_fusion.1
  15.1 0.7 maximum_bitcast_fusion.shard
  15.9 0.9 pad_maximum_fusion.8.x_edges
  16.9 0.6 stack.42.meta
  17.5 0.6 stack.48.params
  18.1 41.0 %first.1 = (bf16[16,16,768]{2,1,0:T(8,128)(2,1)}, bf16[16,16,768]{2,1,0:T(8,128)(2,1)}, bf16[4,2,4,4,24,384]{5,4,3,2,1,0:T(8,128)(2,1)}, f32[16,768]{1,0:T(8,128...) custom-call(s32[6,16]{1,0:T(8,128)} %stack.42.meta, ...), custom_call_target="tpu_custom_call" | custom-call | tf_op jit(solution)/shard_map/first/pallas_call | solution.py:357
  59.1 2.0 slice.166
  61.1 2.9 slice.165
  64.0 1.3 slice_reduce_fusion.4
  65.9 2.9 copy.24
  68.8 69.0 %forward.1 = (bf16[16,128,768]{2,1,0:T(8,128)(2,1)}, f32[16,128,384]{2,1,0:T(8,128)}, bf16[16,128,768]{2,1,0:T(8,128)(2,1)}, bf16[32,32,768]{2,1,0:T(8,128)(2,1)...) custom-call(s32[6,16]{1,0:T(8,128)} %stack.42.meta, bf16[16,128,768]{2,1,0:T(8,128)(2,1)} %x.3, ...), custom_call_target="tpu_custom_call" | custom-call | tf_op jit(solution)/shard_map/forward/pallas_call | solution.py:506
  137.9 29.3 %conditional.1 = ((bf16[32,32,768]{2,1,0:T(8,128)(2,1)S(1)}, bf16[32,32,768]{2,1,0:T(8,128)(2,1)S(1)})) conditional(s32[]{:T(128)} %clamp.3, (bf16[32,32,768]{2,1,0:T(8,128)(2,1)S(1)}, bf16[32,32,768]{2,1,0:T(8,128)(2,1)S(1)}) %tuple.99, (bf16[32,32,768]{2,1,0:T(8,128)(2,1)S(1)}, ...), branch_computations={%region_4.5_spmd, %region_5.6_spmd, %region_6.7_spmd, %region_7.8_... | conditional | flops 1572864 | bytes 27525184 | solution.py:891
  138.1 2.8 collective-permute-start.2
  140.9 26.2 %collective-permute-done.2 = bf16[24,32,768]{2,1,0:T(8,128)(2,1)S(1)} collective-permute-done((bf16[24,32,768]{2,1,0:T(8,128)(2,1)S(1)}, bf16[24,32,768]{2,1,0:T(8,128)(2,1)S(1)}, u32[]{:S(2)}, u32[]{:S(2)}) %collective-permute-start.2) | collective-permute-done | bytes 1179680 | tf_op jit(solution)/shard_map/cond/branch_3_fun/ppermute | solution.py:885
  167.2 110.8 %backward.1 = (bf16[16,128,768]{2,1,0:T(8,128)(2,1)}, bf16[16,16,768]{2,1,0:T(8,128)(2,1)}, bf16[16,16,768]{2,1,0:T(8,128)(2,1)}, bf16[32,32,768]{2,1,0:T(8,128)...) custom-call(s32[6,16]{1,0:T(8,128)} %stack.42.meta, ...), custom_call_target="tpu_custom_call" | custom-call | tf_op jit(solution)/shard_map/backward/pallas_call | solution.py:709
  278.1 0.7 copy-done.3
  278.8 0.6 dynamic_slice.18
  279.4 0.6 dynamic_slice.17
  280.0 0.6 dynamic_slice.19
  280.6 0.6 dynamic_slice.16
  281.2 0.6 dynamic_slice.15
  281.8 13.3 %last.1 = (bf16[16,128,768]{2,1,0:T(8,128)(2,1)}, bf16[16,128,768]{2,1,0:T(8,128)(2,1)}) custom-call(s32[6,16]{1,0:T(8,128)} %stack.42.meta, bf16[16,128,768]{2,1,0:T(8,128)(2,1)} %get-tuple-element.112.grad, bf16[16,16,768]{2,1,0:T(8,128)(2,1)} %get-tuple-element.113.left, bf16[16,16,768]{2,1,0:T(8,128)(2,1)} %get-tuple-element.114.right, ...), custom_call_target="tpu_custom_call" | custom-call | tf_op jit(solution)/shard_map/last/pallas_call | solution.py:784
  295.1 99.2 %reduce-scatter.2.cloned.1.call-done = f32[4,24,384]{2,1,0:T(8,128)} async-done(((f32[4,768,384]{2,1,0:T(8,128)}), f32[4,24,384]{2,1,0:T(8,128)}) %reduce-scatter.2.cloned.1.call-update) | async-done | bytes 147472 | tf_op jit(solution)/shard_map/reduce_scatter | solution.py:917
  394.4 1.4 slice_bitcast_fusion.2
  395.8 1.5 slice.167
  (34 shorter events, 1.1 us)
Async XLA Ops:
  7.2 7.9 %copy-start.1 = (bf16[384,96]{0,1:T(8,128)(2,1)S(1)}, bf16[384,96]{0,1:T(8,128)(2,1)}, u32[]{:S(2)}) copy-start(bf16[384,96]{0,1:T(8,128)(2,1)} %param.28) | copy-start | bytes 221188
  7.2 7.9 %copy-start = (bf16[3,96,384]{2,1,0:T(8,128)(2,1)S(1)}, bf16[3,96,384]{2,1,0:T(8,128)(2,1)}, u32[]{:S(2)}) copy-start(bf16[3,96,384]{2,1,0:T(8,128)(2,1)} %param.25) | copy-start | bytes 663556
  7.2 387.2 %reduce-scatter.2.cloned.1.call-start = ((), (), s32[]{:S(2)}) async-start(), calls=%async_computation.1 | async-start | bytes 4866048 | tf_op jit(solution)/shard_map/reduce_scatter | solution.py:917
  13.8 3.1 copy-start.4
  138.1 29.0 %collective-permute-start.2 = (bf16[24,32,768]{2,1,0:T(8,128)(2,1)S(1)}, bf16[24,32,768]{2,1,0:T(8,128)(2,1)S(1)}, u32[]{:S(2)}, u32[]{:S(2)}) collective-permute-start(bf16[24,32,768]{2,1,0:T(8,128)(2,1)S(1)} %pad_maximum_fusion.2), channel_id=1, source_target_pairs={{0,7},{1,6},{2,5},{3,4},{4,3},{5,2},{6,1},{7,0},{8,15},{9,14},{10,... | collective-permute-start | bytes 3538952 | tf_op jit(solution)/shard_map/cond/branch_3_fun/ppermute | solution.py:885
  278.1 0.7 copy-start.3
  278.1 2.5 copy-start.2
Sparse Core Ops, SparseCore 0:
  278.3 116.0 reduce-scatter.1

commit v2 on v1

--- a/solution.py
+++ b/solution.py
@@ -13,7 +13,7 @@
 EPSILON = 1e-05
 CHUNK = 32
 BASE_SLOTS = 8
-FIRST_SLOTS = 2
+PUMPS = (2, 2, 3, 3, 2, 12, 1, 2, 3)
 WINDOW = 2
 EDGE = 16
 VMEM_LIMIT = 60 * 1024 * 1024
@@ -250,146 +250,6 @@
     return jnp.sum(values.reshape(rows // 8, 8, width), axis=0)
 
 
-def first_kernel(dims, meta, x, x_edges, cot, shard, params, *rest):
-    dp_count, bin_count, seqs, rows, chans, feats, base, first = dims
-    (x_low, x_high, weights, totals, stage, extra, landed_cot) = rest[:7]
-    (sums, own_stage) = rest[7:9]
-    reduce_refs = rest[9:16]
-    (halo_sent, halo_landed, one_sent, one_landed, two_sent, two_landed, three_sent, three_landed, local) = rest[16:25]
-    cot_sent, cot_landed = rest[25:27]
-    place = Place(dp_count, bin_count)
-    per_slot = rows // CHUNK
-    place.barrier()
-
-    halo = Halo(
-        place, x_edges.at[0], x_edges.at[1], x_low, x_high, halo_sent, halo_landed
-    )
-    halo.start()
-    keep = pltpu.make_async_copy(
-        shard.at[place.dp], weights.at[place.chip, place.core, place.dp], local.at[0]
-    )
-    keep.start()
-    ones = []
-    for apart in range(1, place.chip_count):
-        to = lax.rem(place.chip + apart, place.chip_count)
-        ones.append(
-            remote(
-                shard.at[place.dp],
-                weights.at[place.chip, place.core, place.dp],
-                one_sent.at[apart - 1],
-                one_landed.at[apart - 1],
-                (place.dp, to * 2 + place.core),
-            )
-        )
-        ones[-1].start()
-
-    def pack(target, slot, piece, origin):
-        target[slot * per_slot + piece] = cot[meta[2, origin] * per_slot + piece]
-
-    for slot in range(first):
-        for piece in range(per_slot):
-            pack(own_stage, slot, piece, slot)
-    stream = Stream(place, own_stage, landed_cot, cot_sent, cot_landed, first * per_slot)
-
-    sums[...] = jnp.zeros_like(sums)
-    total_bins = rows * bin_count
-    row = lax.broadcasted_iota(jnp.int32, (rows, 1), 0) + place.bin * rows
-
-    def statistics(i):
-        micro = i // (seqs // MICRO)
-        target = row + meta[1, i]
-        inside = jnp.where((target >= 0) & (target < total_bins), 1.0, 0.0).astype(F32)
-        values = x[i].astype(F32) * inside
-        sums[micro] += eighth(values)
-        sums[MICRO + micro] += eighth(values * values)
-
-    lax.fori_loop(0, seqs, lambda i, carry: (statistics(i), carry)[1], 0)
-    mine = reduce_refs[0]
-    mine[0 : 2 * MICRO] = jnp.sum(sums[...], axis=1)
-    mine[2 * MICRO : 4 * MICRO] = params[...]
-    reduce = AllReduce(place, *reduce_refs)
-    reduce.start_near()
-    stream.pump(2)
-
-    for slot in range(first, base):
-        for piece in range(per_slot):
-            pack(stage, slot - first, piece, slot)
-    for slot in range(base, seqs):
-        for piece in range(per_slot):
-            pack(extra, slot - base, piece, slot)
-
-    keep.wait()
-    for copy in ones:
-        copy.wait()
-    twos = []
-    for apart in range(1, dp_count):
-        to = lax.rem(place.dp + apart, dp_count)
-        part = weights.at[:, place.core, place.dp]
-        twos.append(
-            remote(
-                part, part, two_sent.at[apart - 1], two_landed.at[apart - 1], (to, place.bin)
-            )
-        )
-        twos[-1].start()
-    reduce.finish_near()
-    reduce.start_far()
-    stream.pump(2)
-    totals[...] = reduce.finish_far()
-    stream.pump(2)
-    for copy in twos:
-        copy.wait()
-    half = weights.at[:, place.core]
-    three = remote(half, half, three_sent.at[0], three_landed.at[0], (place.dp, place.bin + 1 - 2 * place.core))
-    three.start()
-    stream.pump(2)
-    three.wait()
-    halo.finish()
-    stream.finish()
-
-
-def run_first(dims, meta, x, x_edges, cot, shard, params):
-    dp_count, bin_count, seqs, rows, chans, feats, base, first = dims
-    per_slot = rows // CHUNK
-    quarter = chans // bin_count // dp_count
-    chips = bin_count // 2
-    wshape = (chips, 2, dp_count, TAPS + 1, quarter, feats)
-    dma = pltpu.SemaphoreType.DMA
-    return pl.pallas_call(
-        functools.partial(first_kernel, dims),
-        out_shape=(
-            jax.ShapeDtypeStruct((seqs, EDGE, chans), BF16),
-            jax.ShapeDtypeStruct((seqs, EDGE, chans), BF16),
-            jax.ShapeDtypeStruct(wshape, BF16),
-            jax.ShapeDtypeStruct((4 * MICRO, chans), F32),
-            jax.ShapeDtypeStruct(((base - first) * per_slot, CHUNK, chans), BF16),
-            jax.ShapeDtypeStruct(((seqs - base) * per_slot, CHUNK, chans), BF16),
-            jax.ShapeDtypeStruct((first * per_slot, CHUNK, chans), BF16),
-        ),
-        in_specs=[smem(), vmem(), anywhere(), vmem(), anywhere(), vmem()],
-        out_specs=(vmem(), vmem(), anywhere(), vmem(), vmem(), vmem(), anywhere()),
-        scratch_shapes=[
-            pltpu.VMEM((2 * MICRO, 8, chans), F32),
-            pltpu.VMEM((first * per_slot, CHUNK, chans), BF16),
-            *AllReduce.scratch(dp_count, bin_count, 4 * MICRO, chans),
-            dma((2,)),
-            dma((2,)),
-            dma((chips,)),
-            dma((chips,)),
-            dma((dp_count,)),
-            dma((dp_count,)),
-            dma((1,)),
-            dma((1,)),
-            dma((1,)),
-            dma((first * per_slot,)),
-            dma((first * per_slot,)),
-        ],
-        compiler_params=pltpu.CompilerParams(
-            collective_id=0, has_side_effects=True, vmem_limit_bytes=VMEM_LIMIT
-        ),
-        name="first",
-    )(meta, x, x_edges, cot, shard, params)
-
-
 def norm_rows(totals, gains, count, scale_ref, offset_ref, inverse_ref, shift_ref):
     for micro in range(MICRO):
         mean = totals[micro : micro + 1] / count
@@ -417,32 +277,149 @@
     return value, slope
 
 
-def forward_kernel(dims, meta, x, x_low, x_high, w, proj, totals, stage, *rest):
-    dp_count, bin_count, seqs, rows, chans, feats, base, first = dims
-    (moved, conv, out, out_stage, out_extra, landed_cot, totals_two) = rest[:7]
-    (scale_one, offset_one, scale_two, offset_two, sums) = rest[7:12]
-    reduce_refs = rest[12:19]
-    cot_sent, cot_landed = rest[19:21]
+def front_kernel(dims, meta, x_in, cot, shard, vectors, *rest):
+    dp_count, bin_count, seqs, rows, chans, feats, base = dims
+    (moved_out, conv_out, out_out, out_stage, out_extra, cot_extra, landed_cot, weights_out) = rest[:8]
+    (stats_out, params_out, totals_two) = rest[8:11]
+    (x, x_low, x_high, to_left, to_right, moved, conv, out, w, stage) = rest[11:21]
+    (sums_one, sums, scale_one, offset_one, scale_two, offset_two) = rest[21:27]
+    reduce_first = rest[27:34]
+    reduce_second = rest[34:41]
+    (local, stores, halo_sent, halo_landed, one_sent, one_landed, two_sent, two_landed, three_sent, three_landed) = rest[41:51]
+    cot_sent, cot_landed = rest[51:53]
     place = Place(dp_count, bin_count)
     per_slot = rows // CHUNK
-    pieces = (base - first) * per_slot
+    per_micro = seqs // MICRO
+    share = chans // bin_count
+    group = TAPS + 1
+    total_bins = rows * bin_count
+    load = pltpu.make_async_copy(x_in, x, local.at[0])
+    load.start()
+    tap = lax.rem(place.dp, group)
+    home = pl.ds(pl.multiple_of(place.bin * share, 8), share)
+    keep = pltpu.make_async_copy(shard.at[tap], weights_out.at[tap, home], local.at[1])
+    keep.start()
     place.barrier()
-    stream = Stream(place, stage, landed_cot, cot_sent, cot_landed, pieces)
+
+    ones = []
+    for apart in range(1, place.chip_count):
+        to = lax.rem(place.chip + apart, place.chip_count)
+        ones.append(
+            remote(
+                shard.at[tap],
+                weights_out.at[tap, home],
+                one_sent.at[apart - 1],
+                one_landed.at[apart - 1],
+                (place.dp, to * 2 + place.core),
+            )
+        )
+        ones[-1].start()
+    for slot in range(base):
+        origin = meta[2, slot] * per_slot
+        for piece in range(per_slot):
+            stage[slot * per_slot + piece] = cot[origin + piece]
+    stream = Stream(place, stage, landed_cot, cot_sent, cot_landed, base * per_slot)
     stream.pump(WINDOW)
-    per_micro = seqs // MICRO
+    load.wait()
+    to_left[...] = x[:, :EDGE]
+    to_right[...] = x[:, rows - EDGE :]
+    halo = Halo(place, to_left, to_right, x_low, x_high, halo_sent, halo_landed)
+    halo.start()
+
+    sums_one[...] = jnp.zeros_like(sums_one)
+    row = lax.broadcasted_iota(jnp.int32, (rows, 1), 0) + place.bin * rows
+
+    def statistics(i):
+        micro = i // per_micro
+        target = row + meta[1, i]
+        inside = jnp.where((target >= 0) & (target < total_bins), 1.0, 0.0).astype(F32)
+        values = x[i].astype(F32) * inside
+        sums_one[micro] += eighth(values)
+        sums_one[MICRO + micro] += eighth(values * values)
+
+    stream.loop(seqs, statistics, PUMPS[0])
+    mine = reduce_first[0]
+    mine[0 : 2 * MICRO] = jnp.sum(sums_one[...], axis=1)
+    mine[2 * MICRO :] = jnp.zeros((bin_count, chans), F32)
+    lane = lax.broadcasted_iota(jnp.int32, (1, chans), 1)
+    reversed_count = jnp.int32(0)
+    for i in range(seqs):
+        reversed_count += meta[0, i]
+    at_home = jnp.where(place.dp == 0, 1.0, 0.0).astype(F32)
+    at_first = jnp.where(place.bin == 0, 1.0, 0.0).astype(F32)
+    counts = jnp.where(lane == feats + place.dp, reversed_count.astype(F32) * at_first, 0.0)
+    mine[pl.ds(2 * MICRO + place.bin, 1)] = vectors[...] * at_home + counts
+    reduce = AllReduce(place, *reduce_first)
+    reduce.start_near()
+    stream.pump(PUMPS[1])
+    for slot in range(base, seqs):
+        origin = meta[2, slot] * per_slot
+        for piece in range(per_slot):
+            cot_extra[(slot - base) * per_slot + piece] = cot[origin + piece]
+    reduce.finish_near()
+    reduce.start_far()
+    keep.wait()
+    for copy in ones:
+        copy.wait()
+    twos = []
+    for apart in range(1, group):
+        to = (place.dp // group) * group + lax.rem(tap + apart, group)
+        for chip in range(place.chip_count):
+            part = weights_out.at[tap, pl.ds(pl.multiple_of((chip * 2 + place.core) * share, 8), share)]
+            index = (apart - 1) * place.chip_count + chip
+            twos.append(remote(part, part, two_sent.at[index], two_landed.at[index], (to, place.bin)))
+            twos[-1].start()
+    stream.pump(PUMPS[2])
+    first = reduce.finish_far()
+    stats_out[...] = first[: 2 * MICRO]
+    params_out[...] = jnp.zeros_like(params_out)
+    begin = 0
+    for index, (line, offset, width) in enumerate(
+        ((0, 0, share), (1, 0, share), (2, 0, share), (3, 0, share // 2), (3, feats, share // 2))
+    ):
+        for member in range(bin_count):
+            left = offset + member * width
+            params_out[line : line + 1, left : left + width] = first[
+                2 * MICRO + member : 2 * MICRO + member + 1, begin : begin + width
+            ]
+        begin += width
+    params_out[4:5] = first[2 * MICRO : 2 * MICRO + 1]
+    stream.pump(PUMPS[3])
+    for copy in twos:
+        copy.wait()
+    threes = []
+    for line in range(group):
+        for chip in range(place.chip_count):
+            part = weights_out.at[line, pl.ds(pl.multiple_of((chip * 2 + place.core) * share, 8), share)]
+            index = line * place.chip_count + chip
+            threes.append(
+                remote(
+                    part,
+                    part,
+                    three_sent.at[index],
+                    three_landed.at[index],
+                    (place.dp, place.bin + 1 - 2 * place.core),
+                )
+            )
+            threes[-1].start()
     count = float(per_micro * rows * dp_count * bin_count)
-    stats = totals[...]
-    params = stats[2 * MICRO :]
-    norm_rows(stats, (params[0:1], params[1:2]), count, scale_one, offset_one, None, None)
+    params = params_out[...]
+    norm_rows(first, (params[0:1], params[1:2]), count, scale_one, offset_one, None, None)
     proj_bias = params[2:3]
     sums[...] = jnp.zeros_like(sums)
+    stream.pump(PUMPS[4])
+    halo.finish()
+    for copy in threes:
+        copy.wait()
+    fetch = pltpu.make_async_copy(weights_out, w, local.at[2])
+    fetch.start()
+    fetch.wait()
 
     long_rows = rows + 2 * DILATION
     across = rows + 2 * EDGE
     local_row = lax.broadcasted_iota(jnp.int32, (long_rows, across), 0) - DILATION
     column = lax.broadcasted_iota(jnp.int32, (long_rows, across), 1)
     mask_row = lax.broadcasted_iota(jnp.int32, (long_rows, 1), 0) - DILATION
-    total_bins = rows * bin_count
 
     def up(i):
         micro = i // per_micro
@@ -453,6 +430,7 @@
         source = jnp.concatenate([x_low[i], x[i], x_high[i]], axis=0)
         shifted = matmul(pick, source, 1, 0)
         moved[i] = shifted[DILATION : DILATION + rows].astype(BF16)
+        pltpu.make_async_copy(moved.at[i], moved_out.at[i], stores.at[0]).start()
         hidden = gelu(shifted * scale_one[micro] + offset_one[micro])
         where = place.bin * rows + begin + mask_row * direction
         hidden = jnp.where((where >= 0) & (where < total_bins), hidden, 0.0)
@@ -462,18 +440,19 @@
             term = matmul(window, w[tap], 1, 0)
             result = term if result is None else result + term
         conv[i] = result
+        pltpu.make_async_copy(conv.at[i], conv_out.at[i], stores.at[1]).start()
         sums[micro] += eighth(result)
         sums[MICRO + micro] += eighth(result * result)
 
-    stream.loop(seqs, up, seqs)
-    mine = reduce_refs[0]
+    stream.loop(seqs, up, PUMPS[5])
+    mine = reduce_second[0]
     mine[...] = jnp.sum(sums[...], axis=1)
-    reduce = AllReduce(place, *reduce_refs)
+    reduce = AllReduce(place, *reduce_second)
     reduce.start_near()
-    stream.pump(1)
+    stream.pump(PUMPS[6])
     reduce.finish_near()
     reduce.start_far()
-    stream.pump(2)
+    stream.pump(PUMPS[7])
     stats_two = reduce.finish_far()
     totals_two[...] = stats_two
     norm_rows(
@@ -483,10 +462,11 @@
     def down(i):
         micro = i // per_micro
         hidden = gelu(conv[i] * scale_two[micro] + offset_two[micro]).astype(BF16)
-        branch = matmul(hidden, proj[...], 1, 1) + proj_bias
+        branch = matmul(hidden, w[TAPS], 1, 1) + proj_bias
         out[i] = (moved[i].astype(F32) + branch).astype(BF16)
-
-    stream.loop(seqs, down, seqs)
+        pltpu.make_async_copy(out.at[i], out_out.at[i], stores.at[2]).start()
+
+    stream.loop(seqs, down, PUMPS[8])
     for slot in range(base):
         origin = meta[2, slot]
         for piece in range(per_slot):
@@ -495,47 +475,84 @@
         origin = meta[2, slot]
         for piece in range(per_slot):
             out_extra[(slot - base) * per_slot + piece] = out[origin, piece * CHUNK : (piece + 1) * CHUNK]
+    pltpu.make_async_copy(moved, moved_out, stores.at[0]).wait()
+    pltpu.make_async_copy(conv, conv_out, stores.at[1]).wait()
+    pltpu.make_async_copy(out, out_out, stores.at[2]).wait()
     stream.finish()
 
 
-def run_forward(dims, meta, x, x_low, x_high, w, proj, totals, stage):
-    dp_count, bin_count, seqs, rows, chans, feats, base, first = dims
+def run_front(dims, meta, x, cot, shard, vectors):
+    dp_count, bin_count, seqs, rows, chans, feats, base = dims
     per_slot = rows // CHUNK
-    pieces = (base - first) * per_slot
+    chips = bin_count // 2
+    group = TAPS + 1
     dma = pltpu.SemaphoreType.DMA
+    big = (seqs, rows, chans)
+    packed = jax.ShapeDtypeStruct((base * per_slot, CHUNK, chans), BF16)
+    spare = jax.ShapeDtypeStruct(((seqs - base) * per_slot, CHUNK, chans), BF16)
+    edge = pltpu.VMEM((seqs, EDGE, chans), BF16)
     return pl.pallas_call(
-        functools.partial(forward_kernel, dims),
+        functools.partial(front_kernel, dims),
         out_shape=(
-            jax.ShapeDtypeStruct((seqs, rows, chans), BF16),
+            jax.ShapeDtypeStruct(big, BF16),
             jax.ShapeDtypeStruct((seqs, rows, feats), F32),
-            jax.ShapeDtypeStruct((seqs, rows, chans), BF16),
-            jax.ShapeDtypeStruct((base * per_slot, CHUNK, chans), BF16),
-            jax.ShapeDtypeStruct(((seqs - base) * per_slot, CHUNK, chans), BF16),
-            jax.ShapeDtypeStruct((pieces, CHUNK, chans), BF16),
+            jax.ShapeDtypeStruct(big, BF16),
+            packed,
+            spare,
+            spare,
+            packed,
+            jax.ShapeDtypeStruct((group, chans, feats), BF16),
+            jax.ShapeDtypeStruct((2 * MICRO, chans), F32),
+            jax.ShapeDtypeStruct((8, chans), F32),
             jax.ShapeDtypeStruct((2 * MICRO, feats), F32),
         ),
-        in_specs=[smem(), *[vmem()] * 6, anywhere()],
-        out_specs=(*[vmem()] * 5, anywhere(), vmem()),
+        in_specs=[smem(), anywhere(), vmem(), anywhere(), vmem()],
+        out_specs=(*[anywhere()] * 3, *[vmem()] * 3, anywhere(), anywhere(), *[vmem()] * 3),
         scratch_shapes=[
+            pltpu.VMEM(big, BF16),
+            edge,
+            edge,
+            edge,
+            edge,
+            pltpu.VMEM(big, BF16),
+            pltpu.VMEM((seqs, rows, feats), F32),
+            pltpu.VMEM(big, BF16),
+            pltpu.VMEM((group, chans, feats), BF16),
+            pltpu.VMEM((base * per_slot, CHUNK, chans), BF16),
+            pltpu.VMEM((2 * MICRO, 8, chans), F32),
+            pltpu.VMEM((2 * MICRO, 8, feats), F32),
             pltpu.VMEM((MICRO, 1, chans), F32),
             pltpu.VMEM((MICRO, 1, chans), F32),
             pltpu.VMEM((MICRO, 1, feats), F32),
             pltpu.VMEM((MICRO, 1, feats), F32),
-            pltpu.VMEM((2 * MICRO, 8, feats), F32),
+            *AllReduce.scratch(dp_count, bin_count, 2 * MICRO + bin_count, chans),
             *AllReduce.scratch(dp_count, bin_count, 2 * MICRO, feats),
-            dma((pieces,)),
-            dma((pieces,)),
+            dma((3,)),
+            dma((3,)),
+            dma((2,)),
+            dma((2,)),
+            dma((chips,)),
+            dma((chips,)),
+            dma((TAPS * chips,)),
+            dma((TAPS * chips,)),
+            dma((group * chips,)),
+            dma((group * chips,)),
+            dma((base * per_slot,)),
+            dma((base * per_slot,)),
         ],
         compiler_params=pltpu.CompilerParams(
             collective_id=1, has_side_effects=True, vmem_limit_bytes=VMEM_LIMIT
         ),
-        name="forward",
-    )(meta, x, x_low, x_high, w, proj, totals, stage)
-
-
-def backward_kernel(dims, meta, moved, conv, w, proj, totals, totals_two, cot, cot_a, cot_b, cot_c, out_stage, *rest):
-    dp_count, bin_count, seqs, rows, chans, feats, base, first = dims
-    (grads, low_edge, high_edge, landed_out, sums_two_out, sums_one_out, partial) = rest[:7]
+        name="front",
+    )(meta, x, cot, shard, vectors)
+
+
+def backward_kernel(
+    dims, meta, moved, conv, w, stats_one, params_in, totals_two, cot, cot_near, cot_far, out_stage, *rest
+):
+    dp_count, bin_count, seqs, rows, chans, feats, base = dims
+    own_scatter = scatters(dims)
+    (grads, low_edge, high_edge, landed_out, sums_two_out, sums_one_out, result) = rest[:7]
     (cots, scale_one, offset_one, inverse_one, shift_one) = rest[7:12]
     (scale_two, offset_two, inverse_two, shift_two) = rest[12:16]
     (grad_two, grad_one, hidden_all, cotangents_unused, conv_grad, hidden_group, window_group) = rest[16:23]
@@ -544,14 +561,17 @@
     reduce_two = rest[36:43]
     reduce_one = rest[43:50]
     (local, halo_sent, halo_landed, last_sent, last_landed, out_sent, out_landed) = rest[50:57]
+    partial = result
+    if own_scatter:
+        (partial, halves, dp_send, dp_got, chip_send, chip_got) = rest[57:63]
+        (core_sent, core_landed, dp_sent, dp_landed, chip_sent, chip_landed) = rest[63:69]
     place = Place(dp_count, bin_count)
     per_slot = rows // CHUNK
     per_micro = seqs // MICRO
     loads = [
         pltpu.make_async_copy(cot, cots.at[0:seqs], local.at[0]),
-        pltpu.make_async_copy(cot_a, cots.at[seqs : seqs + first], local.at[1]),
-        pltpu.make_async_copy(cot_b, cots.at[seqs + first : seqs + base], local.at[2]),
-        pltpu.make_async_copy(cot_c, cots.at[seqs + base : 2 * seqs], local.at[3]),
+        pltpu.make_async_copy(cot_near, cots.at[seqs : seqs + base], local.at[1]),
+        pltpu.make_async_copy(cot_far, cots.at[seqs + base : 2 * seqs], local.at[2]),
     ]
     for load in loads:
         load.start()
@@ -559,8 +579,8 @@
     stream = Stream(place, out_stage, landed_out, out_sent, out_landed, base * per_slot)
     stream.pump(WINDOW)
     count = float(per_micro * rows * dp_count * bin_count)
-    stats = totals[...]
-    params = stats[2 * MICRO :]
+    stats = stats_one[...]
+    params = params_in[...]
     stats_two = totals_two[...]
     norm_rows(stats, (params[0:1], params[1:2]), count, scale_one, offset_one, inverse_one, shift_one)
     norm_rows(
@@ -576,6 +596,10 @@
     sums_one[...] = jnp.zeros_like(sums_one)
     bias_sum[...] = jnp.zeros_like(bias_sum)
     partial[...] = jnp.zeros_like(partial)
+
+    def gather(line, term):
+        partial[line] += term.reshape(partial.shape[1:])
+
     for load in loads:
         load.wait()
 
@@ -586,12 +610,12 @@
         values = conv[i]
         hidden, slope = gelu_both(values * scale_two[micro] + offset_two[micro])
         hidden_all[i] = hidden.astype(BF16)
-        grad = matmul(cotangent, proj[...], 1, 0) * slope
+        grad = matmul(cotangent, w[TAPS], 1, 0) * slope
         grad_two[i] = grad
         centred = values * inverse_two[micro] + shift_two[micro]
         sums_two[micro] += eighth(grad)
         sums_two[MICRO + micro] += eighth(grad * centred)
-        partial[TAPS] += matmul(cotangent, hidden_all[i], 0, 0)
+        gather(TAPS, matmul(cotangent, hidden_all[i], 0, 0))
 
     stream.loop(seqs, head, seqs // 2)
     mine = reduce_two[0]
@@ -655,23 +679,47 @@
         sums_one[MICRO + micro] += eighth(grad * centred)
 
     for micro in range(MICRO):
-
-        def one(inner, carry, micro=micro):
-            tail(micro * per_micro + inner)
-            return carry
-
         stream.loop(per_micro, lambda inner, micro=micro: tail(micro * per_micro + inner), per_micro // 2)
         for tap in range(TAPS):
-            partial[tap] += matmul(hidden_group[...], window_group[tap], 0, 0)
+            gather(tap, matmul(hidden_group[...], window_group[tap], 0, 0))
 
     mine = reduce_one[0]
     mine[...] = jnp.sum(sums_one[...], axis=1)
     reduce = AllReduce(place, *reduce_one)
     reduce.start_near()
+    if own_scatter:
+        across = remote(
+            partial.at[:, :, :, 1 - place.core],
+            halves,
+            core_sent.at[0],
+            core_landed.at[0],
+            (place.dp, place.bin + 1 - 2 * place.core),
+        )
+        across.start()
     stream.pump(1)
     reduce.finish_near()
     reduce.start_far()
     stream.pump(2)
+    if own_scatter:
+        across.wait()
+        for target in range(dp_count):
+            for chip in range(place.chip_count):
+                both = partial[:, target, chip, place.core] + halves[:, target, chip]
+                halves[:, target, chip] = both
+                dp_send[target, chip] = both.reshape(dp_send.shape[2:]).astype(BF16)
+        dp_copies = []
+        for apart in range(1, dp_count):
+            to = lax.rem(place.dp + apart, dp_count)
+            dp_copies.append(
+                remote(
+                    dp_send.at[to],
+                    dp_got.at[apart - 1],
+                    dp_sent.at[apart - 1],
+                    dp_landed.at[apart - 1],
+                    (to, place.bin),
+                )
+            )
+            dp_copies[-1].start()
     back_one = reduce.finish_far()
     sums_one_out[...] = back_one
     for micro in range(MICRO):
@@ -693,14 +741,51 @@
     last = Halo(place, last_left, last_right, last_from_left, last_from_right, last_sent, last_landed)
     last.start()
     stream.pump(2)
+    if own_scatter:
+        for copy in dp_copies:
+            copy.wait()
+        for chip in range(place.chip_count):
+            total = halves[:, place.dp, chip].reshape(dp_send.shape[2:])
+            for apart in range(1, dp_count):
+                total += dp_got[apart - 1, chip].astype(F32)
+            chip_send[chip] = total
+        chip_copies = []
+        for apart in range(1, place.chip_count):
+            to = lax.rem(place.chip + apart, place.chip_count)
+            chip_copies.append(
+                remote(
+                    chip_send.at[to],
+                    chip_got.at[apart - 1],
+                    chip_sent.at[apart - 1],
+                    chip_landed.at[apart - 1],
+                    (place.dp, to * 2 + place.core),
+                )
+            )
+            chip_copies[-1].start()
     last.finish()
     low_edge[...] = last_from_left[...]
     high_edge[...] = last_from_right[...]
+    if own_scatter:
+        for copy in chip_copies:
+            copy.wait()
+        total = chip_send[place.chip]
+        for apart in range(1, place.chip_count):
+            total += chip_got[apart - 1]
+        result[...] = total.reshape(result.shape)
     stream.finish()
 
 
-def run_backward(dims, meta, moved, conv, w, proj, totals, totals_two, cot, cot_a, cot_b, cot_c, out_stage):
-    dp_count, bin_count, seqs, rows, chans, feats, base, first = dims
+def scatters(dims):
+    dp_count, bin_count, chans = dims[0], dims[1], dims[4]
+    return chans % (dp_count * bin_count * 8) == 0
+
+
+def run_backward(dims, meta, moved, conv, w, stats_one, params, totals_two, cot, cot_near, cot_far, out_stage):
+    dp_count, bin_count, seqs, rows, chans, feats, base = dims
+    chips = bin_count // 2
+    group = TAPS + 1
+    quarter = chans // (dp_count * bin_count)
+    own_scatter = scatters(dims)
     per_slot = rows // CHUNK
     per_micro = seqs // MICRO
     dma = pltpu.SemaphoreType.DMA
@@ -715,9 +800,9 @@
             jax.ShapeDtypeStruct((base * per_slot, CHUNK, chans), BF16),
             jax.ShapeDtypeStruct((4 * MICRO, feats), F32),
             jax.ShapeDtypeStruct((2 * MICRO, chans), F32),
-            jax.ShapeDtypeStruct((TAPS + 1, chans, feats), F32),
+            jax.ShapeDtypeStruct((group, quarter if own_scatter else chans, feats), F32),
         ),
-        in_specs=[smem(), *[vmem()] * 6, *[anywhere()] * 5],
+        in_specs=[smem(), *[vmem()] * 6, *[anywhere()] * 4],
         out_specs=(vmem(), vmem(), vmem(), anywhere(), vmem(), vmem(), vmem()),
         scratch_shapes=[
             pltpu.VMEM((2 * seqs, rows, chans), BF16),
@@ -752,54 +837,85 @@
             dma((2,)),
             dma((base * per_slot,)),
             dma((base * per_slot,)),
+            *(
+                (
+                    pltpu.VMEM((group, dp_count, chips, 2, quarter, feats), F32),
+                    pltpu.VMEM((group, dp_count, chips, quarter, feats), F32),
+                    pltpu.VMEM((dp_count, chips, group * quarter, feats), BF16),
+                    pltpu.VMEM((dp_count, chips, group * quarter, feats), BF16),
+                    pltpu.VMEM((chips, group * quarter, feats), F32),
+                    pltpu.VMEM((chips, group * quarter, feats), F32),
+                    dma((1,)),
+                    dma((1,)),
+                    dma((dp_count,)),
+                    dma((dp_count,)),
+                    dma((chips,)),
+                    dma((chips,)),
+                )
+                if own_scatter
+                else ()
+            ),
         ],
         compiler_params=pltpu.CompilerParams(
             collective_id=2, has_side_effects=True, vmem_limit_bytes=VMEM_LIMIT
         ),
         name="backward",
-    )(meta, moved, conv, w, proj, totals, totals_two, cot, cot_a, cot_b, cot_c, out_stage)
-
-
-def last_kernel(rows, meta, grad, left, right, out, near, far, result_out, result_grad):
-    i = pl.program_id(0)
-    reverse, shift, slot, near_slots = meta[0, i], meta[1, i], meta[4, i], meta[5, i]
-    crossed = jnp.where(slot < near_slots, near[0], far[0])
-    result_out[0] = jnp.where(reverse > 0, crossed, out[0])
-    low = jnp.where(reverse > 0, right[0], left[0])
-    high = jnp.where(reverse > 0, left[0], right[0])
-    source = jnp.concatenate([low, grad[0], high], axis=0)
+    )(meta, moved, conv, w, stats_one, params, totals_two, cot, cot_near, cot_far, out_stage)
+
+
+def last_kernel(rows, seqs, base, meta, grad, left, right, out, near, far, result_out, result_grad, held, made, got, put):
+    for i in range(seqs):
+        reverse, slot = meta[0, i], meta[4, i]
+
+        @pl.when(reverse == 0)
+        def _():
+            pltpu.make_async_copy(out.at[i], held.at[i], got.at[i]).start()
+
+        @pl.when((reverse > 0) & (slot < base))
+        def _():
+            pltpu.make_async_copy(near.at[jnp.minimum(slot, base - 1)], held.at[i], got.at[i]).start()
+
+        @pl.when((reverse > 0) & (slot >= base))
+        def _():
+            pltpu.make_async_copy(far.at[jnp.maximum(slot - base, 0)], held.at[i], got.at[i]).start()
+
     across = rows + 2 * EDGE
     row = lax.broadcasted_iota(jnp.int32, (rows, across), 0)
     column = lax.broadcasted_iota(jnp.int32, (rows, across), 1)
-    place = jnp.where(reverse > 0, rows - 1 - row - shift, row + shift) + EDGE
-    pick = jnp.where(column == place, 1.0, 0.0).astype(BF16)
-    result_grad[0] = matmul(pick, source, 1, 0).astype(BF16)
+
+    def step(i, carry):
+        reverse, shift = meta[0, i], meta[1, i]
+        low = jnp.where(reverse > 0, right[i], left[i])
+        high = jnp.where(reverse > 0, left[i], right[i])
+        source = jnp.concatenate([low, grad[i], high], axis=0)
+        place = jnp.where(reverse > 0, rows - 1 - row - shift, row + shift) + EDGE
+        pick = jnp.where(column == place, 1.0, 0.0).astype(BF16)
+        made[i] = matmul(pick, source, 1, 0).astype(BF16)
+        pltpu.make_async_copy(made.at[i], result_grad.at[i], put.at[0]).start()
+        pltpu.make_async_copy(held.at[i], held.at[i], got.at[i]).wait()
+        pltpu.make_async_copy(held.at[i], result_out.at[i], put.at[1]).start()
+        return carry
+
+    lax.fori_loop(0, seqs, step, 0)
+    pltpu.make_async_copy(made, result_grad, put.at[0]).wait()
+    pltpu.make_async_copy(held, result_out, put.at[1]).wait()
 
 
 def run_last(dims, meta, grad, left, right, out, near, far):
-    dp_count, bin_count, seqs, rows, chans, feats, base, first = dims
-    full = (1, rows, chans)
-    edge = (1, EDGE, chans)
-    own = lambda i, meta: (i, 0, 0)
+    dp_count, bin_count, seqs, rows, chans, feats, base = dims
+    big = (seqs, rows, chans)
     return pl.pallas_call(
-        functools.partial(last_kernel, rows),
-        out_shape=(
-            jax.ShapeDtypeStruct((seqs, rows, chans), BF16),
-            jax.ShapeDtypeStruct((seqs, rows, chans), BF16),
-        ),
-        grid_spec=pltpu.PrefetchScalarGridSpec(
-            num_scalar_prefetch=1,
-            grid=(seqs,),
-            in_specs=[
-                pl.BlockSpec(full, own),
-                pl.BlockSpec(edge, own),
-                pl.BlockSpec(edge, own),
-                pl.BlockSpec(full, own),
-                pl.BlockSpec(full, lambda i, meta: (jnp.minimum(meta[4, i], base - 1), 0, 0)),
-                pl.BlockSpec(full, lambda i, meta: (jnp.maximum(meta[4, i] - base, 0), 0, 0)),
-            ],
-            out_specs=(pl.BlockSpec(full, own), pl.BlockSpec(full, own)),
-        ),
+        functools.partial(last_kernel, rows, seqs, base),
+        out_shape=(jax.ShapeDtypeStruct(big, BF16), jax.ShapeDtypeStruct(big, BF16)),
+        in_specs=[smem(), vmem(), vmem(), vmem(), anywhere(), anywhere(), anywhere()],
+        out_specs=(anywhere(), anywhere()),
+        scratch_shapes=[
+            pltpu.VMEM(big, BF16),
+            pltpu.VMEM(big, BF16),
+            pltpu.SemaphoreType.DMA((seqs,)),
+            pltpu.SemaphoreType.DMA((2,)),
+        ],
+        compiler_params=pltpu.CompilerParams(vmem_limit_bytes=VMEM_LIMIT),
         name="last",
     )(meta, grad, left, right, out, near, far)
 
@@ -822,8 +938,8 @@
     dp_count, bin_count = lax.axis_size("dp"), lax.axis_size("bins")
     dp, bins = lax.axis_index("dp"), lax.axis_index("bins")
     per_slot = rows // CHUNK
-    base, first = BASE_SLOTS, FIRST_SLOTS
-    dims = (dp_count, bin_count, seqs, rows, chans, feats, base, first)
+    base = BASE_SLOTS
+    dims = (dp_count, bin_count, seqs, rows, chans, feats, base)
 
     reverse = (reverse_flags > 0).astype(jnp.int32)
     index = jnp.arange(seqs, dtype=jnp.int32)
@@ -833,48 +949,25 @@
         jnp.where((slot[None, :] == index[:, None]) & (reverse[None, :] > 0), index[None, :], 0), axis=1
     )
     chosen = jnp.where(reverse > 0, seqs + slot, index)
-    meta = jnp.stack([reverse, shift_bins, origin, chosen, slot, jnp.full((seqs,), base, jnp.int32)])
-    reversed_count = jnp.sum(reverse)
-
-    lane = jnp.arange(chans, dtype=jnp.int32)
-    at_home = dp == 0
-
-    def spread(vector):
-        size = vector.shape[0]
-        width = size * bin_count
-        held = jnp.tile(vector.astype(F32), bin_count)
-        return jnp.where((jnp.arange(width) // size == bins) & at_home, held, 0.0)
-
-    counts = jnp.where((lane == dp) & (bins == 0), reversed_count.astype(F32), 0.0)
-    nothing = jnp.zeros((chans,), F32)
-    params = jnp.stack(
-        [
-            spread(gain_one),
-            spread(bias_one),
-            spread(proj_bias),
-            jnp.concatenate([spread(gain_two), spread(bias_two)]),
-            counts,
-            nothing,
-            nothing,
-            nothing,
-        ]
-    )
-    share = chans // bin_count
-    quarter = share // dp_count
+    meta = jnp.stack([reverse, shift_bins, origin, chosen, slot])
+    vectors = jnp.concatenate([gain_one, bias_one, proj_bias, gain_two, bias_two]).astype(F32)
+    vectors = jnp.pad(vectors, (0, chans - vectors.shape[0]))[None]
     shard = jnp.concatenate([conv_weight, proj_weight.T[None]], axis=0)
-    shard = shard.reshape(TAPS + 1, dp_count, quarter, feats).transpose(1, 0, 2, 3)
-    edges = jnp.stack([activations[:, :EDGE], activations[:, rows - EDGE :]])
-
-    x_low, x_high, weights, totals, stage, cot_extra, cot_a = run_first(
-        dims, meta, activations, edges, cotangent.reshape(seqs * per_slot, CHUNK, chans), shard, params
-    )
-    full = weights.transpose(3, 0, 1, 2, 4, 5).reshape(TAPS + 1, chans, feats)
-    w, proj = full[:TAPS], full[TAPS]
-    most = jnp.max(totals[3 * MICRO, :dp_count]).astype(jnp.int32)
-
-    moved, conv, out, out_stage, out_extra, cot_b, totals_two = run_forward(
-        dims, meta, activations, x_low, x_high, w, proj, totals, stage
-    )
+
+    (
+        moved,
+        conv,
+        out,
+        out_stage,
+        out_extra,
+        cot_extra,
+        cot_near,
+        w,
+        stats_one,
+        params,
+        totals_two,
+    ) = run_front(dims, meta, activations, cotangent.reshape(seqs * per_slot, CHUNK, chans), shard, vectors)
+    most = jnp.max(params[4, feats : feats + dp_count]).astype(jnp.int32)
 
     pairs = [(source, bin_count - 1 - source) for source in range(bin_count)]
 
@@ -901,12 +994,11 @@
         moved,
         conv,
         w,
-        proj,
-        totals,
+        stats_one,
+        params,
         totals_two,
         cotangent,
-        slots_of(cot_a),
-        slots_of(cot_b),
+        slots_of(cot_near),
         slots_of(extra[0]),
         out_stage,
     )
@@ -914,7 +1006,9 @@
         dims, meta, grads, low_edge, high_edge, out, slots_of(out_near), slots_of(extra[1])
     )
 
-    scattered = lax.psum_scatter(partial, ("dp", "bins"), scatter_dimension=1, tiled=True)
+    scattered = partial
+    if not scatters(dims):
+        scattered = lax.psum_scatter(partial, ("dp", "bins"), scatter_dimension=1, tiled=True)
     wide = chans // (dp_count * bin_count)
     narrow = feats // bin_count
     wide_at = (dp * bin_count + bins) * wide

time: 397 us -> 284 us (0.72); the launches traced: 404 us -> 283 us
  waiting for transfers between devices: 125 us -> 26.1 us
  between operations: 15.5 us -> 1.39 us
  local copies, waits for them, and re-layouts: 20.6 us -> 9.65 us
  Pallas kernels: 234 us -> 238 us
    reduce_scatter x1 -> x0, waiting for transfers between devices: 99.2 us -> none  [local(): lax.psum_scatter(partial, ('dp', 'bins'), scatter_dimension=1, tiled=True)]
    pallas_call x1, Pallas kernels: 111 us -> 132 us  [run_backward(): pl.pallas_call(functools.partial(backward_kernel, dims), out_shape=(jax.S...]
    pallas_call x3 -> x2, Pallas kernels: 123 us -> 107 us  [the longest x1 99.4 us: run_front(): pl.pallas_call(functools.partial(front_kernel, dims), out_shape=(jax.Shap...]
    slice x3 -> x0, local copies, waits for them, and re-layouts: 7.75 us -> none  [local(): w, proj = (full[:TAPS], full[TAPS])]
    another operation x16 -> x1, local copies, waits for them, and re-layouts: 6.15 us -> 1.26 us  [local(): meta = jnp.stack([reverse, shift_bins, origin, chosen, slot])]
  transfers between devices with their start and end apart: 2 -> 1, of which waited for: 2 -> 1; matrix products, arithmetic and copies ran while one was open for 1% -> 0% of each run, Pallas kernels for 3% -> 0%
where the time goes in v2:
time: 284 us; the launch traced here: 283 us
  Pallas kernels  238 us (84%)
  waiting for transfers between devices  26.1 us (9%)
  local copies, waits for them, and re-layouts  9.65 us (3%)
  other arithmetic  4.71 us (2%)
  starting transfers between devices  3.1 us (1%)
    pallas_call x1, Pallas kernels, run_backward(): pl.pallas_call(functools.partial(backward_kernel, dims), out_shape=(jax.S...  132 us
    pallas_call x1, Pallas kernels, run_front(): pl.pallas_call(functools.partial(front_kernel, dims), out_shape=(jax.Shap...  99.4 us
    ppermute x1, waiting for transfers between devices, crossing(): lax.ppermute(jnp.concatenate([item[:held] for item in pair]), 'bins', pairs)  26.1 us
    pallas_call x1, Pallas kernels, run_last(): pl.pallas_call(functools.partial(last_kernel, rows, seqs, base), out_shap...  7.1 us
  transfers between devices with their start and end apart: 1, of which 1 were waited for; matrix products, arithmetic and copies ran while one was open for 0% of the time, Pallas kernels for 0%

profile of v2, /device:TPU:0, one launch (start us, length us, event | category | flops | bytes accessed | tf_op | source)
XLA Modules:
  0.0 283.3 jit_solution(6930929298843054336)
XLA Ops:
  0.6 0.7 broadcast_compare_fusion
  1.3 0.1 select_reduce_fusion.1
  1.4 0.7 select_bitcast_fusion
  2.1 0.1 select_reduce_fusion
  2.2 1.3 stack.20.meta
  3.5 1.7 pad_maximum_fusion.8.shard
  5.2 3.4 %concatenate.31 = bf16[384]{0:T(512)(128)(2,1)S(1)} concatenate(bf16[96]{0:T(256)(128)(2,1)} %param.23, bf16[96]{0:T(256)(128)(2,1)} %param.24, bf16[96]{0:T(256)(128)(2,1)} %param.29, bf16[48]{0:T(256)(128)(2,1)} %param.26, bf16[48]{0:T(256)(128)(2,1)} %param.27), dimensions={0} | concatenate | bytes 1536 | tf_op jit(solution)/shard_map/concatenate | solution.py:953
  8.6 0.6 reshape.62.vectors
  9.2 99.4 %front.1 = (bf16[16,128,768]{2,1,0:T(8,128)(2,1)}, f32[16,128,384]{2,1,0:T(8,128)}, bf16[16,128,768]{2,1,0:T(8,128)(2,1)}, bf16[32,32,768]{2,1,0:T(8,128)(2,1)},...) custom-call(s32[5,16]{1,0:T(8,128)} %stack.20.meta, ...), custom_call_target="tpu_custom_call" | custom-call | tf_op jit(solution)/shard_map/front/pallas_call | solution.py:494
  108.7 1.3 slice_reduce_fusion.4
  110.6 29.5 %conditional.1 = ((bf16[32,32,768]{2,1,0:T(8,128)(2,1)S(1)}, bf16[32,32,768]{2,1,0:T(8,128)(2,1)S(1)})) conditional(s32[]{:T(128)} %clamp.3, (bf16[32,32,768]{2,1,0:T(8,128)(2,1)S(1)}, bf16[32,32,768]{2,1,0:T(8,128)(2,1)S(1)}) %tuple.99, (bf16[32,32,768]{2,1,0:T(8,128)(2,1)S(1)}, ...), branch_computations={%region_3.4_spmd, %region_4.5_spmd, %region_5.6_spmd, %region_6.7_... | conditional | flops 1572864 | bytes 27525184 | solution.py:984
  110.7 0.1 pad_maximum_fusion.2
  110.8 3.1 %collective-permute-start.2 = (bf16[24,32,768]{2,1,0:T(8,128)(2,1)S(1)}, bf16[24,32,768]{2,1,0:T(8,128)(2,1)S(1)}, u32[]{:S(2)}, u32[]{:S(2)}) collective-permute-start(bf16[24,32,768]{2,1,0:T(8,128)(2,1)S(1)} %pad_maximum_fusion.2), channel_id=1, source_target_pairs={{0,7},{1,6},{2,5},{3,4},{4,3},{5,2},{6,1},{7,0},{8,15},{9,14},{10,... | collective-permute-start | bytes 3538952 | tf_op jit(solution)/shard_map/cond/branch_3_fun/ppermute | solution.py:978
  113.9 26.1 %collective-permute-done.2 = bf16[24,32,768]{2,1,0:T(8,128)(2,1)S(1)} collective-permute-done((bf16[24,32,768]{2,1,0:T(8,128)(2,1)S(1)}, bf16[24,32,768]{2,1,0:T(8,128)(2,1)S(1)}, u32[]{:S(2)}, u32[]{:S(2)}) %collective-permute-start.2) | collective-permute-done | bytes 1179680 | tf_op jit(solution)/shard_map/cond/branch_3_fun/ppermute | solution.py:978
  140.0 0.1 slice_dynamic-update-slice_fusion.4
  140.1 131.8 %backward.1 = (bf16[16,128,768]{2,1,0:T(8,128)(2,1)}, bf16[16,16,768]{2,1,0:T(8,128)(2,1)}, bf16[16,16,768]{2,1,0:T(8,128)(2,1)}, bf16[32,32,768]{2,1,0:T(8,128)...) custom-call(s32[5,16]{1,0:T(8,128)} %stack.20.meta, ...), custom_call_target="tpu_custom_call" | custom-call | tf_op jit(solution)/shard_map/backward/pallas_call | solution.py:794
  271.9 0.0 copy-start
  271.9 0.0 copy-start.1
  271.9 0.0 copy-start.2
  271.9 7.1 %last.1 = (bf16[16,128,768]{2,1,0:T(8,128)(2,1)}, bf16[16,128,768]{2,1,0:T(8,128)(2,1)}) custom-call(s32[5,16]{1,0:T(8,128)} %stack.20.meta, bf16[16,128,768]{2,1,0:T(8,128)(2,1)} %get-tuple-element.106.grad, bf16[16,16,768]{2,1,0:T(8,128)(2,1)} %get-tuple-element.107.left, bf16[16,16,768]{2,1,0:T(8,128)(2,1)} %get-tuple-element.108.right, ...), custom_call_target="tpu_custom_call" | custom-call | tf_op jit(solution)/shard_map/last/pallas_call | solution.py:907
  279.0 0.0 copy-done
  279.0 0.7 slice.122
  279.7 0.6 slice_bitcast_fusion
  280.3 0.0 copy-done.1
  280.3 0.6 dynamic_slice.15
  280.9 0.6 dynamic_slice.16
  281.5 0.0 copy-done.2
  281.5 0.6 dynamic_slice.19
  282.1 0.6 dynamic_slice.17
  282.7 0.6 dynamic_slice.18
  (7 shorter events, 0.1 us)
Async XLA Ops:
  110.8 29.2 %collective-permute-start.2 = (bf16[24,32,768]{2,1,0:T(8,128)(2,1)S(1)}, bf16[24,32,768]{2,1,0:T(8,128)(2,1)S(1)}, u32[]{:S(2)}, u32[]{:S(2)}) collective-permute-start(bf16[24,32,768]{2,1,0:T(8,128)(2,1)S(1)} %pad_maximum_fusion.2), channel_id=1, source_target_pairs={{0,7},{1,6},{2,5},{3,4},{4,3},{5,2},{6,1},{7,0},{8,15},{9,14},{10,... | collective-permute-start | bytes 3538952 | tf_op jit(solution)/shard_map/cond/branch_3_fun/ppermute | solution.py:978
  271.9 7.1 %copy-start = (f32[4,24,384]{2,1,0:T(8,128)S(1)}, f32[4,24,384]{2,1,0:T(8,128)}, u32[]{:S(2)}) copy-start(f32[4,24,384]{2,1,0:T(8,128)} %get-tuple-element.115) | copy-start | bytes 442372
  271.9 8.4 %copy-start.1 = (f32[8,768]{1,0:T(8,128)S(1)}, f32[8,768]{1,0:T(8,128)}, u32[]{:S(2)}) copy-start(f32[8,768]{1,0:T(8,128)} %get-tuple-element.114) | copy-start | bytes 73732
  271.9 9.6 %copy-start.2 = (f32[16,384]{1,0:T(8,128)S(1)}, f32[16,384]{1,0:T(8,128)}, u32[]{:S(2)}) copy-start(f32[16,384]{1,0:T(8,128)} %get-tuple-element.116) | copy-start | bytes 73732
